TPU v7x, 256 devices: a whole 4x4x8 slice. The times are simulated.
256 devices in a mesh: feat: 8 (over z_hi, core), tok: 32 (over y, z_lo, x).
Axes of the slice: x: 4, y: 4, z: 8 (z_hi: 4, z_lo: 2; z = z_hi * 2 + z_lo), core: 2. Of those that a mesh axis runs over, the one named last changes fastest.
Arguments:
- activations: bfloat16 [8192, 28672], P('tok', 'feat'), may hold values from -160 to 160
- dense_rows: float32 [64, 28672], P(None, 'feat'), may hold values from -6 to 6
- targets: float32 [8192, 64], P('tok'), may hold values from -6 to 6
Outputs:
- pruned_rows: float32 [64, 28672], P(None, 'feat')
All inputs are finite; a program needn't handle non-finite values.
Results may differ from a plain program's by a relative error of at most 0.0055.
Values may be sent and summed in bfloat16 or wider, within the bound.
A program may use at most 64 MiB of HBM per device.

v0:
```python
import math

import jax
import jax.numpy as jnp
from jax import lax
from jax.sharding import PartitionSpec as P

DIN = 28672
ROWS = 64
ITERS = 4


step_size = 0.25
threshold = 0.2
epsilon = 1e-06


def total_of_pieces(shard, axis):
    pieces = lax.all_gather(shard, axis)
    return pieces.sum(axis=0)


def padded_to(lines, devices):
    spare = -lines.shape[0] % devices
    if not spare:
        return lines
    return jnp.concatenate([lines, jnp.zeros((spare, *lines.shape[1:]), lines.dtype)])


def sent_to_all(shard, axis):
    devices = lax.axis_size(axis)
    return lax.all_to_all(
        jnp.broadcast_to(shard[None], (devices, *shard.shape)), axis, 0, 0, tiled=True
    )


def in_order(pieces, dim):
    shape = list(pieces.shape[1:])
    shape[dim] *= pieces.shape[0]
    return jnp.moveaxis(pieces, 0, dim).reshape(shape)


def collect(shard, axis, dim):
    pieces = sent_to_all(shard, axis)
    return in_order(pieces, dim)


def in_blocks(shard, dim, devices):
    shape = shard.shape
    pieces = shard.reshape(*shape[:dim], devices, shape[dim] // devices, *shape[dim + 1 :])
    return jnp.moveaxis(pieces, dim, 0)


def sent_and_summed(shard, axis, dim):
    pieces = in_blocks(shard, dim, lax.axis_size(axis))
    arrived = lax.all_to_all(pieces, axis, split_axis=0, concat_axis=0, tiled=True)
    return arrived.sum(axis=0)


def nested_sum(shard, axes):
    lines = shard.reshape(-1, shard.shape[-1])
    padded = padded_to(lines, lax.axis_size(axes))
    whole = collect(sent_and_summed(padded, axes, 0), axes, 0)
    return lax.slice_in_dim(whole, 0, len(lines)).reshape(shard.shape)


def of_everyone(shard, axis):
    everything = sent_to_all(shard, axis)
    return jnp.sum(everything, axis=0)


def momentum_terms(iterations):
    values = []
    current = 1.0
    for _ in range(iterations):
        upcoming = (1.0 + math.sqrt(1.0 + 4.0 * current * current)) / 2.0
        values.append((current - 1.0) / upcoming)
        current = upcoming
    return values


def shrink_step(advance, gradient, total_square):
    mean_square = total_square / (ROWS * DIN)
    moved = advance - step_size * gradient * lax.rsqrt(mean_square + epsilon)
    return jnp.sign(moved) * jnp.maximum(jnp.abs(moved) - threshold, 0.0)


def token_gradient(residual, activations):
    return lax.dot_general(
        residual, activations, (((0,), (0,)), ((), ())), preferred_element_type=jnp.float32
    )


def shards(activations, dense_rows, targets):
    factor = DIN ** (-0.5)
    momentum = momentum_terms(ITERS)
    weights = dense_rows
    advance = dense_rows
    for iteration in range(ITERS):
        rounded = advance.astype(jnp.bfloat16)
        partial_sum = lax.dot_general(
            activations, rounded, (((1,), (1,)), ((), ())), preferred_element_type=jnp.float32
        )
        summed = total_of_pieces(partial_sum, "feat")
        residual = (factor * summed - targets).astype(jnp.bfloat16)
        gradient = nested_sum(token_gradient(residual, activations), "tok")
        total_square = of_everyone(jnp.sum(gradient * gradient), "feat")
        shrunk = shrink_step(advance, gradient, total_square)
        advance = shrunk + momentum[iteration] * (shrunk - weights)
        weights = shrunk
    return weights


def solution(mesh):
    in_specs = (P("tok", "feat"), P(None, "feat"), P("tok", None))
    out_specs = P(None, "feat")
    return jax.shard_map(shards, mesh=mesh, in_specs=in_specs, out_specs=out_specs, check_vma=False)
```

profile of v0, /device:TPU:1, one launch (start us, length us, event | category | flops | bytes accessed | tf_op | source)
XLA Modules:
  0.0 345.7 jit_solution(6827223440680174024)
XLA Ops:
  3.4 20.0 %all-gather = f32[2048,64]{0,1:T(8,128)S(1)} all-gather(f32[256,64]{0,1:T(8,128)S(1)} %fusion.5), channel_id=2, replica_groups=mesh['feat'=8,'tok'=32] {'feat'}, dimensions={0}, use_global_device_ids=true | all-gather | bytes 589824 | tf_op jit(solution)/shard_map/all_gather | solution.py:19
  26.7 21.9 %all_to_all.64 = f32[32,2,3584]{2,1,0:T(2,128)} all-to-all(f32[32,2,3584]{2,1,0:T(2,128)S(1)} %reshape.40), channel_id=1, replica_groups=mesh['feat'=8,'tok'=32] {'tok'}, dimensions={0} | all-to-all | bytes 1835008 | tf_op jit(solution)/shard_map/all_to_all | solution.py:56
  50.4 19.0 %all_to_all.65 = f32[32,2,3584]{2,1,0:T(2,128)S(1)} all-to-all(f32[32,2,3584]{2,1,0:T(2,128)S(1)} %broadcast_in_dim.16), channel_id=1, replica_groups=mesh['feat'=8,'tok'=32] {'tok'}, dimensions={0} | all-to-all | bytes 1835008 | tf_op jit(solution)/shard_map/all_to_all | solution.py:32
  71.6 13.8 %all_to_all.66 = f32[8,1,1]{2,1,0:T(1,128)S(1)} all-to-all(f32[8,1,1]{2,1,0:T(1,128)S(1)} %broadcast_in_dim.17), channel_id=1, replica_groups=mesh['feat'=8,'tok'=32] {'feat'}, dimensions={0} | all-to-all | bytes 64 | tf_op jit(solution)/shard_map/all_to_all | solution.py:32
  91.3 15.8 %all-gather.1 = f32[2048,64]{0,1:T(8,128)S(1)} all-gather(f32[256,64]{0,1:T(8,128)S(1)} %convolution_bitcast_fusion.2), channel_id=3, replica_groups=mesh['feat'=8,'tok'=32] {'feat'}, dimensions={0}, use_global_device_ids=true | all-gather | bytes 589824 | tf_op jit(solution)/shard_map/all_gather | solution.py:19
  108.8 2.6 reshape.41
  111.5 19.7 %all_to_all.67 = f32[32,2,3584]{2,1,0:T(2,128)} all-to-all(f32[32,2,3584]{2,1,0:T(2,128)} %reshape.41), channel_id=1, replica_groups=mesh['feat'=8,'tok'=32] {'tok'}, dimensions={0} | all-to-all | bytes 1835008 | tf_op jit(solution)/shard_map/all_to_all | solution.py:56
  132.9 19.0 %all_to_all.68 = f32[32,2,3584]{2,1,0:T(2,128)S(1)} all-to-all(f32[32,2,3584]{2,1,0:T(2,128)S(1)} %broadcast_in_dim.18), channel_id=1, replica_groups=mesh['feat'=8,'tok'=32] {'tok'}, dimensions={0} | all-to-all | bytes 1835008 | tf_op jit(solution)/shard_map/all_to_all | solution.py:32
  155.2 12.6 %all_to_all.69 = f32[8,1,1]{2,1,0:T(1,128)S(1)} all-to-all(f32[8,1,1]{2,1,0:T(1,128)S(1)} %broadcast_in_dim.19), channel_id=1, replica_groups=mesh['feat'=8,'tok'=32] {'feat'}, dimensions={0} | all-to-all | bytes 64 | tf_op jit(solution)/shard_map/all_to_all | solution.py:32
  171.4 2.7 mul.116
  174.1 2.5 convolution_bitcast_fusion.1
  176.6 16.0 %all-gather.2 = f32[2048,64]{0,1:T(8,128)S(1)} all-gather(f32[256,64]{0,1:T(8,128)S(1)} %convolution_bitcast_fusion.1), channel_id=4, replica_groups=mesh['feat'=8,'tok'=32] {'feat'}, dimensions={0}, use_global_device_ids=true | all-gather | bytes 589824 | tf_op jit(solution)/shard_map/all_gather | solution.py:19
  194.3 2.7 reshape.42
  197.0 19.8 %all_to_all.70 = f32[32,2,3584]{2,1,0:T(2,128)} all-to-all(f32[32,2,3584]{2,1,0:T(2,128)} %reshape.42), channel_id=1, replica_groups=mesh['feat'=8,'tok'=32] {'tok'}, dimensions={0} | all-to-all | bytes 1835008 | tf_op jit(solution)/shard_map/all_to_all | solution.py:56
  218.5 19.0 %all_to_all.71 = f32[32,2,3584]{2,1,0:T(2,128)S(1)} all-to-all(f32[32,2,3584]{2,1,0:T(2,128)S(1)} %broadcast_in_dim.20), channel_id=1, replica_groups=mesh['feat'=8,'tok'=32] {'tok'}, dimensions={0} | all-to-all | bytes 1835008 | tf_op jit(solution)/shard_map/all_to_all | solution.py:32
  240.6 12.6 %all_to_all.72 = f32[8,1,1]{2,1,0:T(1,128)S(1)} all-to-all(f32[8,1,1]{2,1,0:T(1,128)S(1)} %broadcast_in_dim.21), channel_id=1, replica_groups=mesh['feat'=8,'tok'=32] {'feat'}, dimensions={0} | all-to-all | bytes 64 | tf_op jit(solution)/shard_map/all_to_all | solution.py:32
  256.7 2.8 mul.125
  259.5 3.1 multiply_add_fusion
  263.2 15.8 %all-gather.3 = f32[2048,64]{0,1:T(8,128)S(1)} all-gather(f32[256,64]{0,1:T(8,128)S(1)} %convolution_bitcast_fusion), channel_id=5, replica_groups=mesh['feat'=8,'tok'=32] {'feat'}, dimensions={0}, use_global_device_ids=true | all-gather | bytes 589824 | tf_op jit(solution)/shard_map/all_gather | solution.py:19
  282.5 19.8 %all_to_all.73 = f32[32,2,3584]{2,1,0:T(2,128)} all-to-all(f32[32,2,3584]{2,1,0:T(2,128)S(1)} %reshape.43), channel_id=1, replica_groups=mesh['feat'=8,'tok'=32] {'tok'}, dimensions={0} | all-to-all | bytes 1835008 | tf_op jit(solution)/shard_map/all_to_all | solution.py:56
  304.0 19.0 %all_to_all.74 = f32[32,2,3584]{2,1,0:T(2,128)S(1)} all-to-all(f32[32,2,3584]{2,1,0:T(2,128)S(1)} %broadcast_in_dim.22), channel_id=1, replica_groups=mesh['feat'=8,'tok'=32] {'tok'}, dimensions={0} | all-to-all | bytes 1835008 | tf_op jit(solution)/shard_map/all_to_all | solution.py:32
  325.3 12.6 %all_to_all.75 = f32[8,1,1]{2,1,0:T(1,128)S(1)} all-to-all(f32[8,1,1]{2,1,0:T(1,128)S(1)} %broadcast_in_dim.23), channel_id=1, replica_groups=mesh['feat'=8,'tok'=32] {'feat'}, dimensions={0} | all-to-all | bytes 64 | tf_op jit(solution)/shard_map/all_to_all | solution.py:32
  340.4 2.9 mul.134
  343.2 2.5 maximum_multiply_fusion
  (54 shorter events, 44.3 us)
Async XLA Ops:
  0.0 1.5 copy-start
  1.5 22.1 %copy-start.5 = (f32[256,64]{0,1:T(8,128)S(1)}, f32[256,64]{0,1:T(8,128)}, u32[]{:S(2)}) copy-start(f32[256,64]{0,1:T(8,128)} %param.5) | copy-start | bytes 196612
  151.9 0.9 copy-start.1
  237.5 0.9 copy-start.2
  262.6 16.7 %copy-start.3 = (f32[64,3584]{1,0:T(8,128)}, f32[64,3584]{1,0:T(8,128)S(1)}, u32[]{:S(2)}) copy-start(f32[64,3584]{1,0:T(8,128)S(1)} %multiply_add_fusion) | copy-start | bytes 2752516
  340.4 2.9 copy-start.4
where the time goes:
time: 347 us; the launch traced here: 346 us
  blocking collectives  277 us (80%)
  other arithmetic  27.2 us (8%)
  local copies, waits for them, and re-layouts  26.5 us (8%)
  matrix products  12.3 us (4%)
    all_to_all x8, blocking collectives, sent_to_all(): lax.all_to_all(jnp.broadcast_to(shard[None], (devices, *shard.shape)), ax...  128 us
    all_to_all x4, blocking collectives, sent_and_summed(): lax.all_to_all(pieces, axis, split_axis=0, concat_axis=0, tiled=True)  81.2 us
    all_gather x4, blocking collectives, total_of_pieces(): pieces = lax.all_gather(shard, axis)  67.6 us
    mul x4, local copies, waits for them, and re-layouts, shrink_step(): moved = advance - step_size * gradient * lax.rsqrt(mean_square + epsilon)  10.2 us
    reshape x4, local copies, waits for them, and re-layouts, in_blocks(): shard.reshape(*shape[:dim], devices, shape[dim] // devices, *shape[dim +...  8.77 us

commit v1 on v0

v1 whole, which is shorter than its diff:
```python
import math

import jax
import jax.numpy as jnp
from jax import lax
from jax.experimental import pallas as pl
from jax.experimental.pallas import tpu as pltpu
from jax.sharding import PartitionSpec as P

DIN = 28672
ROWS = 64
ITERS = 4

step_size = 0.25
threshold = 0.2
epsilon = 1e-06

MESH = pl.DeviceIdType.MESH
FEAT = 8
TOK = 32
TOKENS = 256
HALF = TOKENS // 2
COLS = DIN // FEAT
PIECE_ROWS = 8
PIECE_COLS = COLS // 4


def momentum_terms(iterations):
    values = []
    current = 1.0
    for _ in range(iterations):
        upcoming = (1.0 + math.sqrt(1.0 + 4.0 * current * current)) / 2.0
        values.append((current - 1.0) / upcoming)
        current = upcoming
    return values


OFFSETS = sorted(
    [(dy, dz, dx) for dy in range(4) for dz in range(2) for dx in range(4) if (dy, dz, dx) != (0, 0, 0)],
    key=lambda o: -(min(o[0], 4 - o[0]) + o[1] + min(o[2], 4 - o[2])),
)


def kernel(
    act_hbm, dense_hbm, targets_ref, out_ref,
    act, ahead, low, goal,
    partial, pair_in, half_out, half_in, residual,
    pieces, arrived, gathered, square_feat, square_tok, square_part,
    load_sem, sem,
):
    feat = lax.axis_index("feat")
    tok = lax.axis_index("tok")
    core = lax.rem(feat, 2)
    partner = feat + 1 - 2 * core
    y, z, x = tok // 8, lax.rem(tok // 4, 2), lax.rem(tok, 4)

    def tok_at(offset):
        dy, dz, dx = offset
        return lax.rem(y + dy, 4) * 8 + lax.rem(z + dz, 2) * 4 + lax.rem(x + dx, 4)

    barrier = pltpu.get_barrier_semaphore()
    for offset in OFFSETS:
        pl.semaphore_signal(barrier, inc=1, device_id={"tok": tok_at(offset)}, device_id_type=MESH)
    for k in range(1, FEAT):
        pl.semaphore_signal(barrier, inc=1, device_id={"feat": lax.rem(feat + k, FEAT)}, device_id_type=MESH)

    load_dense = pltpu.make_async_copy(dense_hbm, ahead, load_sem.at[0])
    load_act = pltpu.make_async_copy(act_hbm, act, load_sem.at[1])
    load_dense.start()
    load_act.start()
    goal[...] = targets_ref[pl.ds(pl.multiple_of(core * HALF, HALF), HALF), :].T
    load_dense.wait()
    out_ref[...] = ahead[...]
    low[...] = ahead[...].astype(jnp.bfloat16)
    load_act.wait()
    pl.semaphore_wait(barrier, TOK + FEAT - 2)

    momentum = momentum_terms(ITERS)
    factor = DIN ** (-0.5)

    def copy_to(src, dst, send, recv, device):
        copy = pltpu.make_async_remote_copy(
            src_ref=src, dst_ref=dst, send_sem=send, recv_sem=recv, device_id=device, device_id_type=MESH
        )
        copy.start()

    def wait_for(ref, semaphore):
        pltpu.make_async_copy(ref, ref, semaphore).wait()

    def iteration(it, _):
        def s(i):
            return sem.at[it, i]

        product = lax.dot_general(
            low[...], act[...], (((1,), (1,)), ((), ())), preferred_element_type=jnp.float32
        )
        partial[it, 0] = product[:, :HALF]
        partial[it, 1] = product[:, HALF:]
        copy_to(partial.at[it, 1 - core], pair_in.at[it], s(0), s(1), {"feat": partner})
        wait_for(pair_in.at[it], s(1))
        half = partial[it, core] + pair_in[it]
        half_out[it] = half.astype(jnp.bfloat16)
        for k in (2, 1, 3):
            copy_to(half_out.at[it], half_in.at[it, k - 1], s(2), s(3), {"feat": lax.rem(feat + 2 * k, FEAT)})
        wait_for(half_in.at[it], s(3))
        for k in range(3):
            half = half + half_in[it, k].astype(jnp.float32)
        residual[it, core] = (factor * half - goal[...]).astype(jnp.bfloat16)
        copy_to(residual.at[it, core], residual.at[it, core], s(4), s(5), {"feat": partner})
        wait_for(residual.at[it, 1 - core], s(5))
        whole = jnp.concatenate([residual[it, 0], residual[it, 1]], axis=1)

        for dx in (2, 3, 0, 1):
            cx = lax.rem(x + dx, 4)
            columns = pl.ds(pl.multiple_of(cx * PIECE_COLS, 128), PIECE_COLS)
            block = jnp.dot(whole, act[:, columns], preferred_element_type=jnp.float32)
            for g in range(8):
                pieces[it, g * 4 + cx] = block[g * 8 : g * 8 + 8].astype(jnp.bfloat16)
            for offset in OFFSETS:
                if offset[2] == dx:
                    to = tok_at(offset)
                    copy_to(pieces.at[it, to], arrived.at[it, tok], s(6), s(7), {"tok": to})
        arrived[it, tok] = pieces[it, tok]
        wait_for(arrived.at[it, pl.ds(0, TOK - 1)], s(7))

        total = arrived[it, 0].astype(jnp.float32)
        for p in range(1, TOK):
            total = total + arrived[it, p].astype(jnp.float32)
        gathered[it, tok] = total.astype(jnp.bfloat16)
        square = total * total
        lanes = square[:, :128]
        for c in range(1, PIECE_COLS // 128):
            lanes = lanes + square[:, c * 128 : c * 128 + 128]
        square_feat[it, feat] = jnp.sum(lanes, axis=0, keepdims=True)
        for k in range(1, FEAT):
            copy_to(
                square_feat.at[it, feat], square_feat.at[it, feat], s(8), s(9), {"feat": lax.rem(feat + k, FEAT)}
            )
        for offset in OFFSETS:
            copy_to(gathered.at[it, tok], gathered.at[it, tok], s(10), s(11), {"tok": tok_at(offset)})

        wait_for(square_feat.at[it, pl.ds(0, FEAT - 1)], s(9))
        square_tok[it, tok] = jnp.sum(square_feat[it], axis=0)
        for offset in OFFSETS:
            copy_to(square_tok.at[it, tok], square_tok.at[it, tok], s(12), s(13), {"tok": tok_at(offset)})
        wait_for(square_tok.at[it, pl.ds(0, TOK - 1)], s(13))
        wait_for(gathered.at[it, pl.ds(0, TOK - 1)], s(11))

        total_square = jnp.sum(jnp.sum(square_tok[it], axis=0), axis=1, keepdims=True)
        scale = step_size * lax.rsqrt(total_square / (ROWS * DIN) + epsilon)
        m = jnp.float32(momentum[0])
        for i in range(1, ITERS):
            m = jnp.where(it == i, jnp.float32(momentum[i]), m)

        for c in range(4):
            columns = slice(c * PIECE_COLS, (c + 1) * PIECE_COLS)
            for r in range(4):
                rows = slice(r * 16, r * 16 + 16)
                gradient = jnp.concatenate(
                    [gathered[it, 8 * r + c].astype(jnp.float32), gathered[it, 8 * r + 4 + c].astype(jnp.float32)],
                    axis=0,
                )
                moved = ahead[rows, columns] - scale * gradient
                shrunk = moved - jnp.clip(moved, -threshold, threshold)
                advance = shrunk + m * (shrunk - out_ref[rows, columns])
                out_ref[rows, columns] = shrunk
                ahead[rows, columns] = advance
                low[rows, columns] = advance.astype(jnp.bfloat16)

        wait_for(partial.at[it, 0], s(0))
        wait_for(half_in.at[it], s(2))
        wait_for(residual.at[it, 0], s(4))
        wait_for(arrived.at[it, pl.ds(0, TOK - 1)], s(6))
        wait_for(square_feat.at[it, pl.ds(0, FEAT - 1)], s(8))
        wait_for(gathered.at[it, pl.ds(0, TOK - 1)], s(10))
        wait_for(square_tok.at[it, pl.ds(0, TOK - 1)], s(12))
        return 0

    lax.fori_loop(0, ITERS, iteration, 0)


def shards(activations, dense_rows, targets):
    bf16, f32 = jnp.bfloat16, jnp.float32
    return pl.pallas_call(
        kernel,
        out_shape=jax.ShapeDtypeStruct((ROWS, COLS), f32),
        in_specs=[
            pl.BlockSpec(memory_space=pl.ANY),
            pl.BlockSpec(memory_space=pl.ANY),
            pl.BlockSpec(memory_space=pltpu.VMEM),
        ],
        out_specs=pl.BlockSpec(memory_space=pltpu.VMEM),
        scratch_shapes=[
            pltpu.VMEM((TOKENS, COLS), bf16),
            pltpu.VMEM((ROWS, COLS), f32),
            pltpu.VMEM((ROWS, COLS), bf16),
            pltpu.VMEM((ROWS, HALF), f32),
            pltpu.VMEM((ITERS, 2, ROWS, HALF), f32),
            pltpu.VMEM((ITERS, ROWS, HALF), f32),
            pltpu.VMEM((ITERS, ROWS, HALF), bf16),
            pltpu.VMEM((ITERS, 3, ROWS, HALF), bf16),
            pltpu.VMEM((ITERS, 2, ROWS, HALF), bf16),
            pltpu.VMEM((ITERS, TOK, PIECE_ROWS, PIECE_COLS), bf16),
            pltpu.VMEM((ITERS, TOK, PIECE_ROWS, PIECE_COLS), bf16),
            pltpu.VMEM((ITERS, TOK, PIECE_ROWS, PIECE_COLS), bf16),
            pltpu.VMEM((ITERS, FEAT, 1, 128), f32),
            pltpu.VMEM((ITERS, TOK, 1, 128), f32),
            pltpu.VMEM((1, 128), f32),
            pltpu.SemaphoreType.DMA((2,)),
            pltpu.SemaphoreType.DMA((ITERS, 14)),
        ],
        compiler_params=pltpu.CompilerParams(collective_id=0, has_side_effects=True),
    )(activations, dense_rows, targets)


def solution(mesh):
    in_specs = (P("tok", "feat"), P(None, "feat"), P("tok", None))
    out_specs = P(None, "feat")
    return jax.shard_map(shards, mesh=mesh, in_specs=in_specs, out_specs=out_specs, check_vma=False)
```

time: 347 us -> 119 us (0.34)
  blocking collectives: 277 us -> 0 us
  Pallas kernels: 0 us -> 115 us
  other arithmetic: 27.2 us -> 0 us
  local copies, waits for them, and re-layouts: 26.5 us -> 3.76 us
  matrix products: 12.3 us -> 0 us
    all_to_all x12 -> x0, blocking collectives: 209 us -> none  [the longest x8 128 us: sent_to_all(): lax.all_to_all(jnp.broadcast_to(shard[None], (devices, *shard.shape)), ax...]
    pallas_call x0 -> x1, Pallas kernels: none -> 115 us  [shards(): pl.pallas_call(kernel, out_shape=jax.ShapeDtypeStruct((ROWS, COLS), f32),...]
    all_gather x4 -> x0, blocking collectives: 67.6 us -> none  [total_of_pieces(): pieces = lax.all_gather(shard, axis)]
    reduce_sum x16 -> x0, other arithmetic: 15.3 us -> none  [the longest x4 6.36 us: shards(): total_square = of_everyone(jnp.sum(gradient * gradient), 'feat')]
    dot_general x8 -> x0, matrix products: 12.3 us -> none  [the longest x4 6.85 us: shards(): lax.dot_general(activations, rounded, (((1,), (1,)), ((), ())), preferred...]
    mul x4 -> x0, local copies, waits for them, and re-layouts: 10.2 us -> none  [shrink_step(): moved = advance - step_size * gradient * lax.rsqrt(mean_square + epsilon)]
    mul x5 -> x0, other arithmetic: 8.8 us -> none  [the longest x4 6.34 us: shrink_step(): moved = advance - step_size * gradient * lax.rsqrt(mean_square + epsilon)]
    reshape x4 -> x0, local copies, waits for them, and re-layouts: 8.77 us -> none  [in_blocks(): shard.reshape(*shape[:dim], devices, shape[dim] // devices, *shape[dim +...]
where the time goes in v1:
time: 119 us
  Pallas kernels  115 us (97%)
  local copies, waits for them, and re-layouts  3.76 us (3%)
    pallas_call x1, Pallas kernels, shards(): pl.pallas_call(kernel, out_shape=jax.ShapeDtypeStruct((ROWS, COLS), f32),...  115 us
    unnamed x2, local copies, waits for them, and re-layouts  3.76 us

profile of v1, /device:TPU:1, one launch (start us, length us, event | category | flops | bytes accessed | tf_op | source)
XLA Modules:
  0.0 118.9 jit_solution(8856178420920501702)
XLA Ops:
  0.0 1.6 %copy.4.targets_ref = f32[256,64]{1,0:T(8,128)} copy(f32[256,64]{0,1:T(8,128)} %param.5) | data formatting | bytes 131072 | tf_op args[2]
  1.6 115.2 %shard_map.37 = f32[64,3584]{1,0:T(8,128)} custom-call(bf16[256,3584]{1,0:T(8,128)(2,1)} %act_hbm.1, f32[64,3584]{1,0:T(8,128)} %dense_hbm.1, f32[256,64]{1,0:T(8,128)} %copy.4.targets_ref), custom_call_target="tpu_custom_call" | custom-call | tf_op jit(solution)/shard_map/pallas_call | solution.py:184
  116.8 2.2 %copy.6 = f32[64,3584]{1,0:T(8,128)} copy(f32[64,3584]{1,0:T(8,128)} %shard_map.37) | data formatting | bytes 1835008

commit v2 on v1

v2 whole, which is shorter than its diff:
```python
import math

import jax
import jax.numpy as jnp
from jax import lax
from jax.experimental import pallas as pl
from jax.experimental.pallas import tpu as pltpu
from jax.sharding import PartitionSpec as P

DIN = 28672
ROWS = 64
ITERS = 4

step_size = 0.25
threshold = 0.2
epsilon = 1e-06

MESH = pl.DeviceIdType.MESH
FEAT = 8
TOK = 32
TOKENS = 256
HALF = TOKENS // 2
COLS = DIN // FEAT
PIECE_ROWS = 8
PIECE_COLS = COLS // 4


def momentum_terms(iterations):
    values = []
    current = 1.0
    for _ in range(iterations):
        upcoming = (1.0 + math.sqrt(1.0 + 4.0 * current * current)) / 2.0
        values.append((current - 1.0) / upcoming)
        current = upcoming
    return values


def ring(offset, size):
    return min(offset, size - offset)


TOKEN_PEERS = sorted(
    [(dy, dz, dx) for dy in range(4) for dz in range(2) for dx in range(4) if (dy, dz, dx) != (0, 0, 0)],
    key=lambda o: -(ring(o[0], 4) + o[1] + ring(o[2], 4)),
)
LINE_PEERS = sorted(
    [(dz, dc) for dz in range(8) for dc in range(2) if (dz, dc) != (0, 0)], key=lambda o: -ring(o[0], 8) - o[1] / 2
)
PLANE_PEERS = sorted(
    [(dy, dx) for dy in range(4) for dx in range(4) if (dy, dx) != (0, 0)],
    key=lambda o: -(ring(o[0], 4) + ring(o[1], 4)),
)


def kernel(
    act_hbm, dense_hbm, targets_hbm, weights,
    act, ahead, low, targets,
    partial, pair_in, half_out, half_in, residual,
    pieces, arrived, gathered, line_squares, plane_squares,
    load_sem, sem,
):
    load_dense = pltpu.make_async_copy(dense_hbm, ahead, load_sem.at[0])
    load_act = pltpu.make_async_copy(act_hbm, act, load_sem.at[1])
    load_targets = pltpu.make_async_copy(targets_hbm, targets, load_sem.at[2])
    load_dense.start()
    load_act.start()
    load_targets.start()

    feat = lax.axis_index("feat")
    tok = lax.axis_index("tok")
    core = lax.rem(feat, 2)
    partner = feat + 1 - 2 * core
    y, z_lo, x = tok // 8, lax.rem(tok // 4, 2), lax.rem(tok, 4)
    z = (feat // 2) * 2 + z_lo

    def token_peer(offset):
        dy, dz, dx = offset
        return lax.rem(y + dy, 4) * 8 + lax.rem(z_lo + dz, 2) * 4 + lax.rem(x + dx, 4)

    def line_peer(offset):
        dz, dc = offset
        to = lax.rem(z + dz, 8)
        return {"feat": (to // 2) * 2 + lax.rem(core + dc, 2), "tok": y * 8 + lax.rem(to, 2) * 4 + x}

    barrier = pltpu.get_barrier_semaphore()
    for offset in TOKEN_PEERS:
        pl.semaphore_signal(barrier, inc=1, device_id={"tok": token_peer(offset)}, device_id_type=MESH)
    for k in range(1, FEAT):
        pl.semaphore_signal(barrier, inc=1, device_id={"feat": lax.rem(feat + k, FEAT)}, device_id_type=MESH)

    def predict(it):
        product = lax.dot_general(
            low[...], act[...], (((1,), (1,)), ((), ())), preferred_element_type=jnp.float32
        )
        partial[it, 0] = product[:, :HALF]
        partial[it, 1] = product[:, HALF:]

    load_dense.wait()
    weights[...] = ahead[...]
    low[...] = ahead[...].astype(jnp.bfloat16)
    load_act.wait()
    load_targets.wait()
    predict(0)
    pl.semaphore_wait(barrier, TOK + FEAT - 2)

    momentum = momentum_terms(ITERS)
    factor = DIN ** (-0.5)

    def copy_to(src, dst, send, recv, device):
        pltpu.make_async_remote_copy(
            src_ref=src, dst_ref=dst, send_sem=send, recv_sem=recv, device_id=device, device_id_type=MESH
        ).start()

    def wait_for(ref, semaphore):
        pltpu.make_async_copy(ref, ref, semaphore).wait()

    def iteration(it, _):
        def s(i):
            return sem.at[it, i]

        copy_to(partial.at[it, 1 - core], pair_in.at[it], s(0), s(1), {"feat": partner})
        wait_for(pair_in.at[it], s(1))
        half = partial[it, core] + pair_in[it]
        half_out[it] = half.astype(jnp.bfloat16)
        for k in (2, 1, 3):
            copy_to(half_out.at[it], half_in.at[it, k - 1], s(2), s(3), {"feat": lax.rem(feat + 2 * k, FEAT)})
        goal = targets[:, pl.ds(pl.multiple_of(core * HALF, HALF), HALF)]
        wait_for(half_in.at[it], s(3))
        for k in range(3):
            half = half + half_in[it, k].astype(jnp.float32)
        residual[it, core] = (factor * half - goal).astype(jnp.bfloat16)
        copy_to(residual.at[it, core], residual.at[it, core], s(4), s(5), {"feat": partner})
        wait_for(residual.at[it, 1 - core], s(5))
        whole = jnp.concatenate([residual[it, 0], residual[it, 1]], axis=1)

        for dx in (2, 3, 0, 1):
            cx = lax.rem(x + dx, 4)
            columns = pl.ds(pl.multiple_of(cx * PIECE_COLS, 128), PIECE_COLS)
            block = jnp.dot(whole, act[:, columns], preferred_element_type=jnp.float32)
            for g in range(8):
                pieces[it, g * 4 + cx] = block[g * 8 : g * 8 + 8].astype(jnp.bfloat16)
            for offset in TOKEN_PEERS:
                if offset[2] == dx:
                    to = token_peer(offset)
                    copy_to(pieces.at[it, to], arrived.at[it, tok], s(6), s(7), {"tok": to})
        arrived[it, tok] = pieces[it, tok]
        wait_for(arrived.at[it, pl.ds(0, TOK - 1)], s(7))
        total = arrived[it, 0].astype(jnp.float32)
        for p in range(1, TOK):
            total = total + arrived[it, p].astype(jnp.float32)
        gathered[it, tok] = total.astype(jnp.bfloat16)
        square = total * total
        lanes = square[:, :128]
        for c in range(1, PIECE_COLS // 128):
            lanes = lanes + square[:, c * 128 : c * 128 + 128]

        def spread(squares, slot, value, send, recv, devices):
            squares[it, slot] = value
            for device in devices:
                copy_to(squares.at[it, slot], squares.at[it, slot], send, recv, device)

        def collected(squares, recv):
            wait_for(squares.at[it, pl.ds(0, 15)], recv)
            sums = [squares[it, p] for p in range(16)]
            while len(sums) > 1:
                sums = [a + b for a, b in zip(sums[::2], sums[1::2])]
            return sums[0]

        spread(
            line_squares, z * 2 + core, jnp.sum(lanes, axis=0, keepdims=True), s(8), s(9),
            [line_peer(offset) for offset in LINE_PEERS],
        )
        for offset in TOKEN_PEERS:
            copy_to(gathered.at[it, tok], gathered.at[it, tok], s(10), s(11), {"tok": token_peer(offset)})
        spread(
            plane_squares, y * 4 + x, collected(line_squares, s(9)), s(12), s(13),
            [{"tok": token_peer((dy, 0, dx))} for dy, dx in PLANE_PEERS],
        )
        total_square = jnp.sum(collected(plane_squares, s(13)), axis=1, keepdims=True)
        scale = step_size * lax.rsqrt(total_square / (ROWS * DIN) + epsilon)
        m = jnp.float32(momentum[0])
        for i in range(1, ITERS):
            m = jnp.where(it == i, jnp.float32(momentum[i]), m)

        wait_for(gathered.at[it, pl.ds(0, TOK - 1)], s(11))
        for c in range(4):
            columns = slice(c * PIECE_COLS, (c + 1) * PIECE_COLS)
            for r in range(4):
                rows = slice(r * 16, r * 16 + 16)
                gradient = jnp.concatenate(
                    [gathered[it, 8 * r + c].astype(jnp.float32), gathered[it, 8 * r + 4 + c].astype(jnp.float32)],
                    axis=0,
                )
                moved = ahead[rows, columns] - scale * gradient
                shrunk = moved - jnp.clip(moved, -threshold, threshold)
                advance = shrunk + m * (shrunk - weights[rows, columns])
                weights[rows, columns] = shrunk
                ahead[rows, columns] = advance
                low[rows, columns] = advance.astype(jnp.bfloat16)

        @pl.when(it < ITERS - 1)
        def _():
            predict(it + 1)

        wait_for(partial.at[it, 0], s(0))
        wait_for(half_in.at[it], s(2))
        wait_for(residual.at[it, 0], s(4))
        wait_for(arrived.at[it, pl.ds(0, TOK - 1)], s(6))
        wait_for(line_squares.at[it, pl.ds(0, 15)], s(8))
        wait_for(gathered.at[it, pl.ds(0, TOK - 1)], s(10))
        wait_for(plane_squares.at[it, pl.ds(0, 15)], s(12))
        return 0

    lax.fori_loop(0, ITERS, iteration, 0)


def shards(activations, dense_rows, targets):
    bf16, f32 = jnp.bfloat16, jnp.float32
    return pl.pallas_call(
        kernel,
        out_shape=pltpu.VMEM((ROWS, COLS), f32),
        in_specs=[pl.BlockSpec(memory_space=pltpu.HBM)] * 3,
        out_specs=pl.BlockSpec(memory_space=pltpu.VMEM),
        scratch_shapes=[
            pltpu.VMEM((TOKENS, COLS), bf16),
            pltpu.VMEM((ROWS, COLS), f32),
            pltpu.VMEM((ROWS, COLS), bf16),
            pltpu.VMEM((ROWS, TOKENS), f32),
            pltpu.VMEM((ITERS, 2, ROWS, HALF), f32),
            pltpu.VMEM((ITERS, ROWS, HALF), f32),
            pltpu.VMEM((ITERS, ROWS, HALF), bf16),
            pltpu.VMEM((ITERS, 3, ROWS, HALF), bf16),
            pltpu.VMEM((ITERS, 2, ROWS, HALF), bf16),
            pltpu.VMEM((ITERS, TOK, PIECE_ROWS, PIECE_COLS), bf16),
            pltpu.VMEM((ITERS, TOK, PIECE_ROWS, PIECE_COLS), bf16),
            pltpu.VMEM((ITERS, TOK, PIECE_ROWS, PIECE_COLS), bf16),
            pltpu.VMEM((ITERS, 16, 1, 128), f32),
            pltpu.VMEM((ITERS, 16, 1, 128), f32),
            pltpu.SemaphoreType.DMA((3,)),
            pltpu.SemaphoreType.DMA((ITERS, 14)),
        ],
        compiler_params=pltpu.CompilerParams(collective_id=0, has_side_effects=True),
    )(activations, dense_rows, targets.T)


def solution(mesh):
    in_specs = (P("tok", "feat"), P(None, "feat"), P("tok", None))
    out_specs = P(None, "feat")
    return jax.shard_map(shards, mesh=mesh, in_specs=in_specs, out_specs=out_specs, check_vma=False)
```

time: 119 us -> 111 us (0.933)
  Pallas kernels: 115 us -> 110 us
  local copies, waits for them, and re-layouts: 3.76 us -> 0.93 us
    pallas_call x1, Pallas kernels: 115 us -> 110 us  [shards(): pl.pallas_call(kernel, out_shape=pltpu.VMEM((ROWS, COLS), f32), in_specs=...]
    unnamed x2 -> x1, local copies, waits for them, and re-layouts: 3.76 us -> 0.93 us
where the time goes in v2:
time: 111 us; the launch traced here: 110 us
  Pallas kernels  110 us (99%)
    pallas_call x1, Pallas kernels, shards(): pl.pallas_call(kernel, out_shape=pltpu.VMEM((ROWS, COLS), f32), in_specs=...  110 us

profile of v2, /device:TPU:1, one launch (start us, length us, event | category | flops | bytes accessed | tf_op | source)
XLA Modules:
  0.0 110.5 jit_solution(12840384093454637740)
XLA Ops:
  0.0 109.5 %shard_map.37 = f32[64,3584]{1,0:T(8,128)S(1)} custom-call(bf16[256,3584]{1,0:T(8,128)(2,1)} %act_hbm.1, f32[64,3584]{1,0:T(8,128)} %dense_hbm.1, f32[64,256]{1,0:T(8,128)} %bitcast.1), custom_call_target="tpu_custom_call" | custom-call | tf_op jit(solution)/shard_map/pallas_call | solution.py:219
  109.6 0.9 copy.5

commit v3 on v2

v3 whole, which is shorter than its diff:
```python
import math

import jax
import jax.numpy as jnp
from jax import lax
from jax.experimental import pallas as pl
from jax.experimental.pallas import tpu as pltpu
from jax.sharding import PartitionSpec as P

DIN = 28672
ROWS = 64
ITERS = 4

step_size = 0.25
threshold = 0.2
epsilon = 1e-06

MESH = pl.DeviceIdType.MESH
FEAT = 8
TOK = 32
TOKENS = 256
HALF = ROWS // 2
COLS = DIN // FEAT
PIECE_ROWS = 8
PIECE_COLS = COLS // 4
TILES = PIECE_COLS // 128


def momentum_terms(iterations):
    values = []
    current = 1.0
    for _ in range(iterations):
        upcoming = (1.0 + math.sqrt(1.0 + 4.0 * current * current)) / 2.0
        values.append((current - 1.0) / upcoming)
        current = upcoming
    return values


def ring(offset, size):
    return min(offset, size - offset)


TOKEN_PEERS = sorted(
    [(dy, dz, dx) for dy in range(4) for dz in range(2) for dx in range(4) if (dy, dz, dx) != (0, 0, 0)],
    key=lambda o: -(ring(o[0], 4) + o[1] + ring(o[2], 4)),
)
LINE_PEERS = sorted(
    [(dz, dc) for dz in range(8) for dc in range(2) if (dz, dc) != (0, 0)], key=lambda o: -ring(o[0], 8) - o[1] / 2
)
PLANE_PEERS = sorted(
    [(dy, dx) for dy in range(4) for dx in range(4) if (dy, dx) != (0, 0)],
    key=lambda o: -(ring(o[0], 4) + ring(o[1], 4)),
)


COLUMN_PEERS = sorted([(dz, dx) for dz in range(2) for dx in range(4)], key=lambda o: -(o[0] + ring(o[1], 4)))


def kernel(
    act_hbm, dense_hbm, targets_hbm, weights,
    act, dense, goal, kept, ahead, pair_out, pair_in, product, half_out, half_in,
    pieces, arrived, gathered, line_squares, plane_squares,
    load_sem, pair_sem, sem,
):
    feat = lax.axis_index("feat")
    tok = lax.axis_index("tok")
    core = lax.rem(feat, 2)
    other = 1 - core
    partner = feat + 1 - 2 * core
    y, z_lo, x = tok // 8, lax.rem(tok // 4, 2), lax.rem(tok, 4)
    z = (feat // 2) * 2 + z_lo
    my_rows = pl.ds(pl.multiple_of(core * HALF, HALF), HALF)
    other_rows = pl.ds(pl.multiple_of(other * HALF, HALF), HALF)

    load_dense = pltpu.make_async_copy(dense_hbm, dense, load_sem.at[0])
    load_act = pltpu.make_async_copy(act_hbm, act.at[core], load_sem.at[1])
    load_goal = pltpu.make_async_copy(targets_hbm.at[my_rows], goal, load_sem.at[2])
    load_dense.start()
    load_act.start()
    load_goal.start()

    def token_peer(offset):
        dy, dz, dx = offset
        return lax.rem(y + dy, 4) * 8 + lax.rem(z_lo + dz, 2) * 4 + lax.rem(x + dx, 4)

    def line_peer(offset):
        dz, dc = offset
        to = lax.rem(z + dz, 8)
        return {"feat": (to // 2) * 2 + lax.rem(core + dc, 2), "tok": y * 8 + lax.rem(to, 2) * 4 + x}

    barrier = pltpu.get_barrier_semaphore()
    for offset in TOKEN_PEERS:
        pl.semaphore_signal(barrier, inc=1, device_id={"tok": token_peer(offset)}, device_id_type=MESH)
    for k in range(1, FEAT):
        pl.semaphore_signal(barrier, inc=1, device_id={"feat": lax.rem(feat + k, FEAT)}, device_id_type=MESH)

    def copy_to(src, dst, send, recv, device):
        pltpu.make_async_remote_copy(
            src_ref=src, dst_ref=dst, send_sem=send, recv_sem=recv, device_id=device, device_id_type=MESH
        ).start()

    def wait_for(ref, semaphore):
        pltpu.make_async_copy(ref, ref, semaphore).wait()

    contract_last = (((1,), (1,)), ((), ()))
    momentum = momentum_terms(ITERS)
    factor = DIN ** (-0.5)

    load_dense.wait()
    load_act.wait()
    first = lax.dot_general(
        dense[...].astype(jnp.bfloat16), act[core], contract_last, preferred_element_type=jnp.float32
    )
    pair_out[0] = first[:HALF]
    pair_out[1] = first[HALF:]
    kept[core] = dense[my_rows]
    ahead[core] = dense[my_rows]
    load_goal.wait()
    pl.semaphore_wait(barrier, TOK + FEAT - 2)
    copy_to(pair_out.at[other], pair_in, pair_sem.at[0], pair_sem.at[1], {"feat": partner})
    wait_for(pair_in, pair_sem.at[1])
    product[...] = pair_out[core] + pair_in[...]

    def iteration(it, _):
        def s(i):
            return sem.at[it, i]

        half = product[...]
        half_out[it] = half.astype(jnp.bfloat16)
        for k in (2, 1, 3):
            copy_to(half_out.at[it], half_in.at[it, k - 1], s(0), s(1), {"feat": lax.rem(feat + 2 * k, FEAT)})

        @pl.when(it == 0)
        def _():
            copy_to(act.at[core], act.at[core], pair_sem.at[2], pair_sem.at[3], {"feat": partner})
            copy_to(dense.at[other_rows], kept.at[core], pair_sem.at[4], pair_sem.at[5], {"feat": partner})

        wait_for(half_in.at[it], s(1))
        for k in range(3):
            half = half + half_in[it, k].astype(jnp.float32)
        residual = (factor * half - goal[...]).astype(jnp.bfloat16)

        @pl.when(it == 0)
        def _():
            wait_for(act.at[other], pair_sem.at[3])
            wait_for(kept.at[other], pair_sem.at[5])
            ahead[other] = kept[other]

        for dz, dx in COLUMN_PEERS:
            block, cx = lax.rem(z_lo + dz, 2), lax.rem(x + dx, 4)
            columns = pl.ds(pl.multiple_of(cx * PIECE_COLS, 128), PIECE_COLS)
            part = jnp.dot(residual, act[block, :, columns], preferred_element_type=jnp.float32)
            for g in range(4):
                pieces[it, g * 8 + block * 4 + cx] = part[g * 8 : g * 8 + 8].astype(jnp.bfloat16)
            for dy in (2, 1, 3, 0):
                if (dy, dz, dx) != (0, 0, 0):
                    to = token_peer((dy, dz, dx))
                    copy_to(pieces.at[it, to], arrived.at[it, tok], s(2), s(3), {"tok": to})
        arrived[it, tok] = pieces[it, tok]
        wait_for(arrived.at[it, pl.ds(0, TOK - 1)], s(3))
        total = arrived[it, 0].astype(jnp.float32)
        for p in range(1, TOK):
            total = total + arrived[it, p].astype(jnp.float32)
        gathered[it, tok] = total.astype(jnp.bfloat16)
        square = total * total
        lanes = square[:, :128]
        for c in range(1, TILES):
            lanes = lanes + square[:, c * 128 : c * 128 + 128]

        def spread(squares, slot, value, send, recv, devices):
            squares[it, slot] = value
            for device in devices:
                copy_to(squares.at[it, slot], squares.at[it, slot], send, recv, device)

        def collected(squares, recv):
            wait_for(squares.at[it, pl.ds(0, 15)], recv)
            sums = [squares[it, p] for p in range(16)]
            while len(sums) > 1:
                sums = [a + b for a, b in zip(sums[::2], sums[1::2])]
            return sums[0]

        spread(
            line_squares, z * 2 + core, jnp.sum(lanes, axis=0, keepdims=True), s(4), s(5),
            [line_peer(offset) for offset in LINE_PEERS],
        )
        for offset in TOKEN_PEERS:
            copy_to(gathered.at[it, tok], gathered.at[it, tok], s(6), s(7), {"tok": token_peer(offset)})
        spread(
            plane_squares, y * 4 + x, collected(line_squares, s(5)), s(8), s(9),
            [{"tok": token_peer((dy, 0, dx))} for dy, dx in PLANE_PEERS],
        )
        total_square = jnp.sum(collected(plane_squares, s(9)), axis=1, keepdims=True)
        scale = step_size * lax.rsqrt(total_square / (ROWS * DIN) + epsilon)
        m = jnp.float32(momentum[0])
        for i in range(1, ITERS):
            m = jnp.where(it == i, jnp.float32(momentum[i]), m)
        wait_for(gathered.at[it, pl.ds(0, TOK - 1)], s(7))

        def gradient_tile(block, r, t):
            tiles = [
                gathered[it, (2 * r + g) * 8 + block * 4 + t // TILES, :, (t % TILES) * 128 : (t % TILES) * 128 + 128]
                for g in range(2)
            ]
            return jnp.concatenate([tile.astype(jnp.float32) for tile in tiles], axis=0)

        def shrunk_tile(block, rows, columns, gradient):
            moved = ahead[block, rows, columns] - scale * gradient
            return moved - jnp.clip(moved, -threshold, threshold)

        @pl.when(it < ITERS - 1)
        def _():
            total = None
            for block in range(2):
                for chunk in range(7):
                    low = []
                    for r in range(2):
                        rows = slice(r * 16, r * 16 + 16)
                        line = []
                        for t in range(chunk * 4, chunk * 4 + 4):
                            columns = slice(t * 128, t * 128 + 128)
                            shrunk = shrunk_tile(block, rows, columns, gradient_tile(block, r, t))
                            advance = shrunk + m * (shrunk - kept[block, rows, columns])
                            kept[block, rows, columns] = shrunk
                            ahead[block, rows, columns] = advance
                            line.append(advance.astype(jnp.bfloat16))
                        low.append(jnp.concatenate(line, axis=1))
                    part = lax.dot_general(
                        jnp.concatenate(low, axis=0), act[block, :, chunk * 512 : chunk * 512 + 512],
                        contract_last, preferred_element_type=jnp.float32,
                    )
                    total = part if total is None else total + part
            product[...] = total

        @pl.when(it == ITERS - 1)
        def _():
            def finish(block, target, row_start, t):
                for r in range(2):
                    rows, columns = slice(r * 16, r * 16 + 16), slice(t * 128, t * 128 + 128)
                    shrunk = shrunk_tile(block, rows, columns, gradient_tile(block, r, t))
                    start = row_start + r * 16
                    if not isinstance(start, int):
                        start = pl.multiple_of(start, 16)
                    target[pl.ds(start, 16), columns] = shrunk

            for part in range(4):
                columns = pl.ds(part * PIECE_COLS, PIECE_COLS)
                for t in range(part * TILES, part * TILES + TILES):
                    finish(other, kept.at[other], 0, t)
                copy_to(
                    kept.at[other, :, columns], weights.at[my_rows, columns],
                    pair_sem.at[6], pair_sem.at[7], {"feat": partner},
                )
            for t in range(4 * TILES):
                finish(core, weights, core * HALF, t)
            wait_for(kept.at[core], pair_sem.at[7])
            wait_for(kept.at[core], pair_sem.at[6])

        wait_for(half_in.at[it], s(0))
        wait_for(arrived.at[it, pl.ds(0, TOK - 1)], s(2))
        wait_for(line_squares.at[it, pl.ds(0, 15)], s(4))
        wait_for(gathered.at[it, pl.ds(0, TOK - 1)], s(6))
        wait_for(plane_squares.at[it, pl.ds(0, 15)], s(8))
        return 0

    lax.fori_loop(0, ITERS, iteration, 0)
    wait_for(pair_in, pair_sem.at[0])
    wait_for(act.at[0], pair_sem.at[2])
    wait_for(kept.at[0], pair_sem.at[4])


def shards(activations, dense_rows, targets):
    bf16, f32 = jnp.bfloat16, jnp.float32
    piece_buffer = pltpu.VMEM((ITERS, TOK, PIECE_ROWS, PIECE_COLS), bf16)
    return pl.pallas_call(
        kernel,
        out_shape=pltpu.VMEM((ROWS, COLS), f32),
        in_specs=[pl.BlockSpec(memory_space=pltpu.HBM)] * 3,
        out_specs=pl.BlockSpec(memory_space=pltpu.VMEM),
        scratch_shapes=[
            pltpu.VMEM((2, TOKENS, COLS), bf16),
            pltpu.VMEM((ROWS, COLS), f32),
            pltpu.VMEM((HALF, TOKENS), f32),
            pltpu.VMEM((2, HALF, COLS), f32),
            pltpu.VMEM((2, HALF, COLS), f32),
            pltpu.VMEM((2, HALF, TOKENS), f32),
            pltpu.VMEM((HALF, TOKENS), f32),
            pltpu.VMEM((HALF, TOKENS), f32),
            pltpu.VMEM((ITERS, HALF, TOKENS), bf16),
            pltpu.VMEM((ITERS, 3, HALF, TOKENS), bf16),
            piece_buffer,
            piece_buffer,
            piece_buffer,
            pltpu.VMEM((ITERS, 16, 1, 128), f32),
            pltpu.VMEM((ITERS, 16, 1, 128), f32),
            pltpu.SemaphoreType.DMA((3,)),
            pltpu.SemaphoreType.DMA((8,)),
            pltpu.SemaphoreType.DMA((ITERS, 10)),
        ],
        compiler_params=pltpu.CompilerParams(collective_id=0, has_side_effects=True),
    )(activations, dense_rows, targets.T)


def solution(mesh):
    in_specs = (P("tok", "feat"), P(None, "feat"), P("tok", None))
    out_specs = P(None, "feat")
    return jax.shard_map(shards, mesh=mesh, in_specs=in_specs, out_specs=out_specs, check_vma=False)
```

time: 111 us -> 105 us (0.946)
  Pallas kernels: 110 us -> 104 us
    pallas_call x1, Pallas kernels: 110 us -> 104 us  [shards(): pl.pallas_call(kernel, out_shape=pltpu.VMEM((ROWS, COLS), f32), in_specs=...]
where the time goes in v3:
time: 105 us
  Pallas kernels  104 us (99%)
    pallas_call x1, Pallas kernels, shards(): pl.pallas_call(kernel, out_shape=pltpu.VMEM((ROWS, COLS), f32), in_specs=...  104 us

profile of v3, /device:TPU:1, one launch (start us, length us, event | category | flops | bytes accessed | tf_op | source)
XLA Modules:
  0.0 104.7 jit_solution(11769429442389331496)
XLA Ops:
  0.0 103.8 %shard_map.37 = f32[64,3584]{1,0:T(8,128)S(1)} custom-call(bf16[256,3584]{1,0:T(8,128)(2,1)} %act_hbm.1, f32[64,3584]{1,0:T(8,128)} %dense_hbm.1, f32[64,256]{1,0:T(8,128)} %bitcast.1), custom_call_target="tpu_custom_call" | custom-call | tf_op jit(solution)/shard_map/pallas_call | solution.py:274
  103.8 0.9 copy.5

commit v4 on v0

v4 whole, which is shorter than its diff:
```python
import math

import jax
import jax.numpy as jnp
from jax import lax
from jax.experimental import pallas as pl
from jax.experimental.pallas import tpu as pltpu
from jax.sharding import PartitionSpec as P

DIN = 28672
ROWS = 64
ITERS = 4

step_size = 0.25
threshold = 0.2
epsilon = 1e-06

MESH = pl.DeviceIdType.MESH
FEAT = 8
TOK = 32
TOKENS = 256
COLS = DIN // FEAT
PIECE_ROWS = 16
PIECE_COLS = COLS // 4
TILES = PIECE_COLS // 128


def momentum_terms(iterations):
    values = []
    current = 1.0
    for _ in range(iterations):
        upcoming = (1.0 + math.sqrt(1.0 + 4.0 * current * current)) / 2.0
        values.append((current - 1.0) / upcoming)
        current = upcoming
    return values


def ring(offset, size):
    return min(offset, size - offset)


TOKEN_PEERS = sorted(
    [(dy, dz, dx) for dy in range(4) for dz in range(2) for dx in range(4) if (dy, dz, dx) != (0, 0, 0)],
    key=lambda o: -(ring(o[0], 4) + o[1] + ring(o[2], 4)),
)
LINE_PEERS = sorted(range(1, 8), key=lambda o: -ring(o, 8))
PLANE_PEERS = sorted(
    [(dy, dx) for dy in range(4) for dx in range(4) if (dy, dx) != (0, 0)],
    key=lambda o: -(ring(o[0], 4) + ring(o[1], 4)),
)


COLUMN_PEERS = sorted([(dz, dx) for dz in range(2) for dx in range(4)], key=lambda o: -(o[0] + ring(o[1], 4)))


def kernel(
    act_hbm, dense_hbm, targets_hbm, weights,
    act, goal, kept, ahead, pair_out, pair_in, product, part_out, part_in,
    pieces, arrived, gathered, line_squares, plane_squares,
    load_sem, pair_sem, sem,
):
    feat = lax.axis_index("feat")
    tok = lax.axis_index("tok")
    core = lax.rem(feat, 2)
    partner = {"feat": feat + 1 - 2 * core}

    load_dense = pltpu.make_async_copy(dense_hbm, kept.at[core], load_sem.at[0])
    load_act = pltpu.make_async_copy(act_hbm, act.at[core], load_sem.at[1])
    load_goal = pltpu.make_async_copy(targets_hbm, goal, load_sem.at[2])
    load_dense.start()
    load_act.start()
    load_goal.start()

    barrier = pltpu.get_barrier_semaphore()
    pl.semaphore_signal(barrier, inc=1, device_id=partner, device_id_type=MESH)

    def copy_to(src, dst, send, recv, device):
        pltpu.make_async_remote_copy(
            src_ref=src, dst_ref=dst, send_sem=send, recv_sem=recv, device_id=device, device_id_type=MESH
        ).start()

    def wait_for(ref, semaphore):
        pltpu.make_async_copy(ref, ref, semaphore).wait()

    contract_last = (((1,), (1,)), ((), ()))

    def first_product():
        load_dense.wait()
        load_act.wait()
        load_goal.wait()
        return lax.dot_general(
            kept[core].astype(jnp.bfloat16), act[core], contract_last, preferred_element_type=jnp.float32
        )

    @pl.when(core == 0)
    def _():
        pair_out[...] = first_product()
        pl.semaphore_wait(barrier, 1)
        copy_to(pair_out, pair_in, pair_sem.at[0], pair_sem.at[1], partner)
        copy_to(act.at[0], act.at[0], pair_sem.at[2], pair_sem.at[3], partner)
        copy_to(kept.at[0], kept.at[0], pair_sem.at[4], pair_sem.at[5], partner)
        wait_for(pair_out, pair_sem.at[0])
        wait_for(act.at[0], pair_sem.at[2])
        wait_for(kept.at[0], pair_sem.at[4])
        wait_for(kept.at[0], pair_sem.at[7])

    @pl.when(core == 1)
    def _():
        y, z_lo, x = tok // 8, lax.rem(tok // 4, 2), lax.rem(tok, 4)
        z = (feat // 2) * 2 + z_lo

        def token_peer(offset):
            dy, dz, dx = offset
            return lax.rem(y + dy, 4) * 8 + lax.rem(z_lo + dz, 2) * 4 + lax.rem(x + dx, 4)

        def line_peer(dz):
            to = lax.rem(z + dz, 8)
            return {"feat": (to // 2) * 2 + 1, "tok": y * 8 + lax.rem(to, 2) * 4 + x}

        for offset in TOKEN_PEERS:
            pl.semaphore_signal(barrier, inc=1, device_id={"tok": token_peer(offset)}, device_id_type=MESH)
        for k in (2, 1, 3):
            pl.semaphore_signal(
                barrier, inc=1, device_id={"feat": lax.rem(feat + 2 * k, FEAT)}, device_id_type=MESH
            )
        momentum = momentum_terms(ITERS)
        factor = DIN ** (-0.5)
        product[...] = first_product()
        ahead[1] = kept[1]
        pl.semaphore_wait(barrier, TOK + FEAT // 2 - 1)
        wait_for(pair_in, pair_sem.at[1])
        product[...] += pair_in[...]

        def iteration(it, _):
            def s(i):
                return sem.at[it, i]

            own = product[...]
            part_out[it] = own.astype(jnp.bfloat16)
            for k in (2, 1, 3):
                copy_to(part_out.at[it], part_in.at[it, k - 1], s(0), s(1), {"feat": lax.rem(feat + 2 * k, FEAT)})
            wait_for(part_in.at[it], s(1))
            for k in range(3):
                own = own + part_in[it, k].astype(jnp.float32)
            residual = (factor * own - goal[...]).astype(jnp.bfloat16)

            @pl.when(it == 0)
            def _():
                wait_for(act.at[0], pair_sem.at[3])

            for dz, dx in COLUMN_PEERS:
                block, cx = lax.rem(z_lo + dz, 2), lax.rem(x + dx, 4)
                columns = pl.ds(pl.multiple_of(cx * PIECE_COLS, 128), PIECE_COLS)
                part = jnp.dot(residual, act[block, :, columns], preferred_element_type=jnp.float32)
                for g in range(4):
                    pieces[it, g * 8 + block * 4 + cx] = part[g * 16 : g * 16 + 16].astype(jnp.bfloat16)
                for dy in (2, 1, 3, 0):
                    if (dy, dz, dx) != (0, 0, 0):
                        to = token_peer((dy, dz, dx))
                        copy_to(pieces.at[it, to], arrived.at[it, tok], s(2), s(3), {"tok": to})
            arrived[it, tok] = pieces[it, tok]

            @pl.when(it == 0)
            def _():
                wait_for(kept.at[0], pair_sem.at[5])
                ahead[0] = kept[0]

            wait_for(arrived.at[it, pl.ds(0, TOK - 1)], s(3))
            total = arrived[it, 0].astype(jnp.float32)
            for p in range(1, TOK):
                total = total + arrived[it, p].astype(jnp.float32)
            gathered[it, tok] = total.astype(jnp.bfloat16)
            square = total * total
            square = square[:8] + square[8:]
            lanes = square[:, :128]
            for c in range(1, TILES):
                lanes = lanes + square[:, c * 128 : c * 128 + 128]

            def spread(squares, slot, value, send, recv, devices):
                squares[it, slot] = value
                for device in devices:
                    copy_to(squares.at[it, slot], squares.at[it, slot], send, recv, device)

            def collected(squares, recv, number):
                wait_for(squares.at[it, pl.ds(0, number - 1)], recv)
                sums = [squares[it, p] for p in range(number)]
                while len(sums) > 1:
                    sums = [a + b for a, b in zip(sums[::2], sums[1::2])]
                return sums[0]

            spread(
                line_squares, z, jnp.sum(lanes, axis=0, keepdims=True), s(4), s(5),
                [line_peer(dz) for dz in LINE_PEERS],
            )
            for offset in TOKEN_PEERS:
                copy_to(gathered.at[it, tok], gathered.at[it, tok], s(6), s(7), {"tok": token_peer(offset)})
            spread(
                plane_squares, y * 4 + x, collected(line_squares, s(5), 8), s(8), s(9),
                [{"tok": token_peer((dy, 0, dx))} for dy, dx in PLANE_PEERS],
            )
            total_square = jnp.sum(collected(plane_squares, s(9), 16), axis=1, keepdims=True)
            scale = step_size * lax.rsqrt(total_square / (ROWS * DIN) + epsilon)
            m = jnp.float32(momentum[0])
            for i in range(1, ITERS):
                m = jnp.where(it == i, jnp.float32(momentum[i]), m)
            wait_for(gathered.at[it, pl.ds(0, TOK - 1)], s(7))

            def shrunk_tile(block, r, t):
                rows, columns = slice(r * 16, r * 16 + 16), slice(t * 128, t * 128 + 128)
                inner = slice((t % TILES) * 128, (t % TILES) * 128 + 128)
                gradient = gathered[it, r * 8 + block * 4 + t // TILES, :, inner].astype(jnp.float32)
                moved = ahead[block, rows, columns] - scale * gradient
                return rows, columns, moved - jnp.clip(moved, -threshold, threshold)

            @pl.when(it < ITERS - 1)
            def _():
                total = None
                for block in range(2):
                    for chunk in range(7):
                        low = []
                        for r in range(4):
                            line = []
                            for t in range(chunk * 4, chunk * 4 + 4):
                                rows, columns, shrunk = shrunk_tile(block, r, t)
                                advance = shrunk + m * (shrunk - kept[block, rows, columns])
                                kept[block, rows, columns] = shrunk
                                ahead[block, rows, columns] = advance
                                line.append(advance.astype(jnp.bfloat16))
                            low.append(jnp.concatenate(line, axis=1))
                        part = lax.dot_general(
                            jnp.concatenate(low, axis=0), act[block, :, chunk * 512 : chunk * 512 + 512],
                            contract_last, preferred_element_type=jnp.float32,
                        )
                        total = part if total is None else total + part
                product[...] = total

            @pl.when(it == ITERS - 1)
            def _():
                for part in range(4):
                    block_columns = pl.ds(part * PIECE_COLS, PIECE_COLS)
                    for t in range(part * TILES, part * TILES + TILES):
                        for r in range(4):
                            rows, columns, shrunk = shrunk_tile(0, r, t)
                            kept[0, rows, columns] = shrunk
                    copy_to(
                        kept.at[0, :, block_columns], weights.at[:, block_columns],
                        pair_sem.at[6], pair_sem.at[7], partner,
                    )
                for t in range(4 * TILES):
                    for r in range(4):
                        rows, columns, shrunk = shrunk_tile(1, r, t)
                        weights[rows, columns] = shrunk
                wait_for(kept.at[0], pair_sem.at[6])

            wait_for(part_in.at[it], s(0))
            wait_for(arrived.at[it, pl.ds(0, TOK - 1)], s(2))
            wait_for(line_squares.at[it, pl.ds(0, 7)], s(4))
            wait_for(gathered.at[it, pl.ds(0, TOK - 1)], s(6))
            wait_for(plane_squares.at[it, pl.ds(0, 15)], s(8))
            return 0

        lax.fori_loop(0, ITERS, iteration, 0)


def shards(activations, dense_rows, targets):
    bf16, f32 = jnp.bfloat16, jnp.float32
    piece_buffer = pltpu.VMEM((ITERS, TOK, PIECE_ROWS, PIECE_COLS), bf16)
    return pl.pallas_call(
        kernel,
        out_shape=pltpu.VMEM((ROWS, COLS), f32),
        in_specs=[pl.BlockSpec(memory_space=pltpu.HBM)] * 3,
        out_specs=pl.BlockSpec(memory_space=pltpu.VMEM),
        scratch_shapes=[
            pltpu.VMEM((2, TOKENS, COLS), bf16),
            pltpu.VMEM((ROWS, TOKENS), f32),
            pltpu.VMEM((2, ROWS, COLS), f32),
            pltpu.VMEM((2, ROWS, COLS), f32),
            pltpu.VMEM((ROWS, TOKENS), f32),
            pltpu.VMEM((ROWS, TOKENS), f32),
            pltpu.VMEM((ROWS, TOKENS), f32),
            pltpu.VMEM((ITERS, ROWS, TOKENS), bf16),
            pltpu.VMEM((ITERS, 3, ROWS, TOKENS), bf16),
            piece_buffer,
            piece_buffer,
            piece_buffer,
            pltpu.VMEM((ITERS, 8, 1, 128), f32),
            pltpu.VMEM((ITERS, 16, 1, 128), f32),
            pltpu.SemaphoreType.DMA((3,)),
            pltpu.SemaphoreType.DMA((8,)),
            pltpu.SemaphoreType.DMA((ITERS, 10)),
        ],
        compiler_params=pltpu.CompilerParams(collective_id=0, has_side_effects=True),
    )(activations, dense_rows, targets.T)


def solution(mesh):
    in_specs = (P("tok", "feat"), P(None, "feat"), P("tok", None))
    out_specs = P(None, "feat")
    return jax.shard_map(shards, mesh=mesh, in_specs=in_specs, out_specs=out_specs, check_vma=False)
```

time: 347 us -> 106 us (0.31)
  blocking collectives: 277 us -> 0 us
  Pallas kernels: 0 us -> 105 us
  other arithmetic: 27.2 us -> 0 us
  local copies, waits for them, and re-layouts: 26.5 us -> 0.93 us
  matrix products: 12.3 us -> 0 us
    all_to_all x12 -> x0, blocking collectives: 209 us -> none  [the longest x8 128 us: sent_to_all(): lax.all_to_all(jnp.broadcast_to(shard[None], (devices, *shard.shape)), ax...]
    pallas_call x0 -> x1, Pallas kernels: none -> 105 us  [shards(): pl.pallas_call(kernel, out_shape=pltpu.VMEM((ROWS, COLS), f32), in_specs=...]
    all_gather x4 -> x0, blocking collectives: 67.6 us -> none  [total_of_pieces(): pieces = lax.all_gather(shard, axis)]
    reduce_sum x16 -> x0, other arithmetic: 15.3 us -> none  [the longest x4 6.36 us: shards(): total_square = of_everyone(jnp.sum(gradient * gradient), 'feat')]
    dot_general x8 -> x0, matrix products: 12.3 us -> none  [the longest x4 6.85 us: shards(): lax.dot_general(activations, rounded, (((1,), (1,)), ((), ())), preferred...]
    mul x4 -> x0, local copies, waits for them, and re-layouts: 10.2 us -> none  [shrink_step(): moved = advance - step_size * gradient * lax.rsqrt(mean_square + epsilon)]
    mul x5 -> x0, other arithmetic: 8.8 us -> none  [the longest x4 6.34 us: shrink_step(): moved = advance - step_size * gradient * lax.rsqrt(mean_square + epsilon)]
    reshape x4 -> x0, local copies, waits for them, and re-layouts: 8.77 us -> none  [in_blocks(): shard.reshape(*shape[:dim], devices, shape[dim] // devices, *shape[dim +...]
where the time goes in v4:
time: 106 us
  Pallas kernels  105 us (99%)
    pallas_call x1, Pallas kernels, shards(): pl.pallas_call(kernel, out_shape=pltpu.VMEM((ROWS, COLS), f32), in_specs=...  105 us

profile of v4, /device:TPU:1, one launch (start us, length us, event | category | flops | bytes accessed | tf_op | source)
XLA Modules:
  0.0 105.5 jit_solution(5748134354809880506)
XLA Ops:
  0.0 104.6 %shard_map.37 = f32[64,3584]{1,0:T(8,128)S(1)} custom-call(bf16[256,3584]{1,0:T(8,128)(2,1)} %act_hbm.1, f32[64,3584]{1,0:T(8,128)} %dense_hbm.1, f32[64,256]{1,0:T(8,128)} %bitcast.1), custom_call_target="tpu_custom_call" | custom-call | tf_op jit(solution)/shard_map/pallas_call | solution.py:268
  104.6 0.9 copy.5

commit v5 on v4

--- a/solution.py
+++ b/solution.py
@@ -15,6 +15,8 @@
 threshold = 0.2
 epsilon = 1e-06
 
+RS_N, RS_S = (2, 1), (3, 0)
+AG_N, AG_S = (2,), (1, 3, 0)
 MESH = pl.DeviceIdType.MESH
 FEAT = 8
 TOK = 32
@@ -55,13 +57,15 @@
 
 def kernel(
     act_hbm, dense_hbm, targets_hbm, weights,
-    act, goal, kept, ahead, pair_out, pair_in, product, part_out, part_in,
+    act, goal, kept, ahead, pair_out, pair_in, product, part_out, part_in, residual,
     pieces, arrived, gathered, line_squares, plane_squares,
     load_sem, pair_sem, sem,
 ):
     feat = lax.axis_index("feat")
     tok = lax.axis_index("tok")
     core = lax.rem(feat, 2)
+    y, z_lo, x = tok // 8, lax.rem(tok // 4, 2), lax.rem(tok, 4)
+    z = (feat // 2) * 2 + z_lo
     partner = {"feat": feat + 1 - 2 * core}
 
     load_dense = pltpu.make_async_copy(dense_hbm, kept.at[core], load_sem.at[0])
@@ -91,6 +95,32 @@
         return lax.dot_general(
             kept[core].astype(jnp.bfloat16), act[core], contract_last, preferred_element_type=jnp.float32
         )
+
+    def token_peer(offset):
+        dy, dz, dx = offset
+        return lax.rem(y + dy, 4) * 8 + lax.rem(z_lo + dz, 2) * 4 + lax.rem(x + dx, 4)
+
+    def send_pieces(it, offsets):
+        residuals = jnp.concatenate([residual[it, lax.rem(y + dy, 4)] for dy in offsets], axis=0)
+        for dz, dx in COLUMN_PEERS:
+            block, cx = lax.rem(z_lo + dz, 2), lax.rem(x + dx, 4)
+            columns = pl.ds(pl.multiple_of(cx * PIECE_COLS, 128), PIECE_COLS)
+            part = jnp.dot(residuals, act[block, :, columns], preferred_element_type=jnp.float32)
+            for i, dy in enumerate(offsets):
+                to = token_peer((dy, dz, dx))
+                pieces[it, to] = part[i * 16 : i * 16 + 16].astype(jnp.bfloat16)
+                copy_to(
+                    pieces.at[it, to], arrived.at[it, tok], sem.at[it, 2], sem.at[it, 3],
+                    {"feat": feat + 1 - core, "tok": to} if (dy, dz, dx) != (0, 0, 0) else partner,
+                )
+
+    def send_gradient(it, offsets):
+        for offset in TOKEN_PEERS:
+            if offset[0] in offsets:
+                copy_to(
+                    gathered.at[it, tok], gathered.at[it, tok], sem.at[it, 6], sem.at[it, 7],
+                    {"feat": feat + 1 - core, "tok": token_peer(offset)},
+                )
 
     @pl.when(core == 0)
     def _():
@@ -101,18 +131,23 @@
         copy_to(kept.at[0], kept.at[0], pair_sem.at[4], pair_sem.at[5], partner)
         wait_for(pair_out, pair_sem.at[0])
         wait_for(act.at[0], pair_sem.at[2])
+        wait_for(act.at[1], pair_sem.at[3])
+
+        def help_out(it, _):
+            wait_for(residual.at[it], sem.at[it, 11])
+            send_pieces(it, RS_S)
+            wait_for(gathered.at[it, tok], sem.at[it, 13])
+            send_gradient(it, AG_S)
+            wait_for(pieces.at[it, pl.ds(0, 8 * len(RS_S))], sem.at[it, 2])
+            wait_for(gathered.at[it, pl.ds(0, 8 * len(AG_S) - (0 in AG_S))], sem.at[it, 6])
+            return 0
+
+        lax.fori_loop(0, ITERS, help_out, 0)
         wait_for(kept.at[0], pair_sem.at[4])
         wait_for(kept.at[0], pair_sem.at[7])
 
     @pl.when(core == 1)
     def _():
-        y, z_lo, x = tok // 8, lax.rem(tok // 4, 2), lax.rem(tok, 4)
-        z = (feat // 2) * 2 + z_lo
-
-        def token_peer(offset):
-            dy, dz, dx = offset
-            return lax.rem(y + dy, 4) * 8 + lax.rem(z_lo + dz, 2) * 4 + lax.rem(x + dx, 4)
-
         def line_peer(dz):
             to = lax.rem(z + dz, 8)
             return {"feat": (to // 2) * 2 + 1, "tok": y * 8 + lax.rem(to, 2) * 4 + x}
@@ -128,6 +163,7 @@
         product[...] = first_product()
         ahead[1] = kept[1]
         pl.semaphore_wait(barrier, TOK + FEAT // 2 - 1)
+        copy_to(act.at[1], act.at[1], pair_sem.at[2], pair_sem.at[3], partner)
         wait_for(pair_in, pair_sem.at[1])
         product[...] += pair_in[...]
 
@@ -142,30 +178,23 @@
             wait_for(part_in.at[it], s(1))
             for k in range(3):
                 own = own + part_in[it, k].astype(jnp.float32)
-            residual = (factor * own - goal[...]).astype(jnp.bfloat16)
+            left = (factor * own - goal[...]).astype(jnp.bfloat16)
+            for g in range(4):
+                residual[it, g] = left[g * 16 : g * 16 + 16]
+            copy_to(residual.at[it], residual.at[it], s(10), s(11), partner)
 
             @pl.when(it == 0)
             def _():
                 wait_for(act.at[0], pair_sem.at[3])
 
-            for dz, dx in COLUMN_PEERS:
-                block, cx = lax.rem(z_lo + dz, 2), lax.rem(x + dx, 4)
-                columns = pl.ds(pl.multiple_of(cx * PIECE_COLS, 128), PIECE_COLS)
-                part = jnp.dot(residual, act[block, :, columns], preferred_element_type=jnp.float32)
-                for g in range(4):
-                    pieces[it, g * 8 + block * 4 + cx] = part[g * 16 : g * 16 + 16].astype(jnp.bfloat16)
-                for dy in (2, 1, 3, 0):
-                    if (dy, dz, dx) != (0, 0, 0):
-                        to = token_peer((dy, dz, dx))
-                        copy_to(pieces.at[it, to], arrived.at[it, tok], s(2), s(3), {"tok": to})
-            arrived[it, tok] = pieces[it, tok]
+            send_pieces(it, RS_N)
 
             @pl.when(it == 0)
             def _():
                 wait_for(kept.at[0], pair_sem.at[5])
                 ahead[0] = kept[0]
 
-            wait_for(arrived.at[it, pl.ds(0, TOK - 1)], s(3))
+            wait_for(arrived.at[it], s(3))
             total = arrived[it, 0].astype(jnp.float32)
             for p in range(1, TOK):
                 total = total + arrived[it, p].astype(jnp.float32)
@@ -192,8 +221,8 @@
                 line_squares, z, jnp.sum(lanes, axis=0, keepdims=True), s(4), s(5),
                 [line_peer(dz) for dz in LINE_PEERS],
             )
-            for offset in TOKEN_PEERS:
-                copy_to(gathered.at[it, tok], gathered.at[it, tok], s(6), s(7), {"tok": token_peer(offset)})
+            copy_to(gathered.at[it, tok], gathered.at[it, tok], s(12), s(13), partner)
+            send_gradient(it, AG_N)
             spread(
                 plane_squares, y * 4 + x, collected(line_squares, s(5), 8), s(8), s(9),
                 [{"tok": token_peer((dy, 0, dx))} for dy, dx in PLANE_PEERS],
@@ -253,13 +282,16 @@
                 wait_for(kept.at[0], pair_sem.at[6])
 
             wait_for(part_in.at[it], s(0))
-            wait_for(arrived.at[it, pl.ds(0, TOK - 1)], s(2))
+            wait_for(pieces.at[it, pl.ds(0, 8 * len(RS_N))], s(2))
             wait_for(line_squares.at[it, pl.ds(0, 7)], s(4))
-            wait_for(gathered.at[it, pl.ds(0, TOK - 1)], s(6))
+            wait_for(gathered.at[it, pl.ds(0, 8 * len(AG_N) - (0 in AG_N))], s(6))
+            wait_for(residual.at[it], s(10))
+            wait_for(gathered.at[it, tok], s(12))
             wait_for(plane_squares.at[it, pl.ds(0, 15)], s(8))
             return 0
 
         lax.fori_loop(0, ITERS, iteration, 0)
+        wait_for(act.at[1], pair_sem.at[2])
 
 
 def shards(activations, dense_rows, targets):
@@ -280,6 +312,7 @@
             pltpu.VMEM((ROWS, TOKENS), f32),
             pltpu.VMEM((ITERS, ROWS, TOKENS), bf16),
             pltpu.VMEM((ITERS, 3, ROWS, TOKENS), bf16),
+            pltpu.VMEM((ITERS, 4, 16, TOKENS), bf16),
             piece_buffer,
             piece_buffer,
             piece_buffer,
@@ -287,7 +320,7 @@
             pltpu.VMEM((ITERS, 16, 1, 128), f32),
             pltpu.SemaphoreType.DMA((3,)),
             pltpu.SemaphoreType.DMA((8,)),
-            pltpu.SemaphoreType.DMA((ITERS, 10)),
+            pltpu.SemaphoreType.DMA((ITERS, 14)),
         ],
         compiler_params=pltpu.CompilerParams(collective_id=0, has_side_effects=True),
     )(activations, dense_rows, targets.T)

time: 106 us -> 103 us (0.972)
  Pallas kernels: 105 us -> 102 us
    pallas_call x1, Pallas kernels: 105 us -> 102 us  [shards(): pl.pallas_call(kernel, out_shape=pltpu.VMEM((ROWS, COLS), f32), in_specs=...]
where the time goes in v5:
time: 103 us
  Pallas kernels  102 us (99%)
    pallas_call x1, Pallas kernels, shards(): pl.pallas_call(kernel, out_shape=pltpu.VMEM((ROWS, COLS), f32), in_specs=...  102 us

profile of v5, /device:TPU:1, one launch (start us, length us, event | category | flops | bytes accessed | tf_op | source)
XLA Modules:
  0.0 102.7 jit_solution(12109308168252296006)
XLA Ops:
  0.0 101.8 %shard_map.37 = f32[64,3584]{1,0:T(8,128)S(1)} custom-call(bf16[256,3584]{1,0:T(8,128)(2,1)} %act_hbm.1, f32[64,3584]{1,0:T(8,128)} %dense_hbm.1, f32[64,256]{1,0:T(8,128)} %bitcast.1), custom_call_target="tpu_custom_call" | custom-call | tf_op jit(solution)/shard_map/pallas_call | solution.py:300
  101.8 0.9 copy.5

commit v6 on v5

v6 whole, which is shorter than its diff:
```python
import math

import jax
import jax.numpy as jnp
from jax import lax
from jax.experimental import pallas as pl
from jax.experimental.pallas import tpu as pltpu
from jax.sharding import PartitionSpec as P

DIN = 28672
ROWS = 64
ITERS = 4

step_size = 0.25
threshold = 0.2
epsilon = 1e-06

AG_N, AG_S = (2,), (1, 3, 0)
MESH = pl.DeviceIdType.MESH
FEAT = 8
TOK = 32
TOKENS = 256
COLS = DIN // FEAT
PIECE_ROWS = 16
PIECE_COLS = COLS // 4
TILES = PIECE_COLS // 128


def momentum_terms(iterations):
    values = []
    current = 1.0
    for _ in range(iterations):
        upcoming = (1.0 + math.sqrt(1.0 + 4.0 * current * current)) / 2.0
        values.append((current - 1.0) / upcoming)
        current = upcoming
    return values


def ring(offset, size):
    return min(offset, size - offset)


TOKEN_PEERS = sorted(
    [(dy, dz, dx) for dy in range(4) for dz in range(2) for dx in range(4) if (dy, dz, dx) != (0, 0, 0)],
    key=lambda o: -(ring(o[0], 4) + o[1] + ring(o[2], 4)),
)
LINE_PEERS = sorted(range(1, 8), key=lambda o: -ring(o, 8))
PLANE_PEERS = sorted(
    [(dy, dx) for dy in range(4) for dx in range(4) if (dy, dx) != (0, 0)],
    key=lambda o: -(ring(o[0], 4) + ring(o[1], 4)),
)


COLUMN_PEERS = sorted([(dz, dx) for dz in range(2) for dx in range(4)], key=lambda o: -(o[0] + ring(o[1], 4)))


def kernel(
    act_hbm, dense_hbm, targets_hbm, weights,
    act, goal, kept, ahead, pair_out, pair_in, product, part_out, part_in, residual,
    pieces, arrived, gathered, line_squares, plane_squares, plane_sum,
    load_sem, pair_sem, sem,
):
    feat = lax.axis_index("feat")
    tok = lax.axis_index("tok")
    core = lax.rem(feat, 2)
    y, z_lo, x = tok // 8, lax.rem(tok // 4, 2), lax.rem(tok, 4)
    z = (feat // 2) * 2 + z_lo
    partner = {"feat": feat + 1 - 2 * core}

    def token_peer(offset):
        dy, dz, dx = offset
        return lax.rem(y + dy, 4) * 8 + lax.rem(z_lo + dz, 2) * 4 + lax.rem(x + dx, 4)

    barrier = pltpu.get_barrier_semaphore()

    @pl.when(core == 1)
    def _():
        for offset in TOKEN_PEERS:
            pl.semaphore_signal(barrier, inc=1, device_id={"tok": token_peer(offset)}, device_id_type=MESH)
        for k in (2, 1, 3):
            pl.semaphore_signal(
                barrier, inc=1, device_id={"feat": lax.rem(feat + 2 * k, FEAT)}, device_id_type=MESH
            )

    pl.semaphore_signal(barrier, inc=1, device_id=partner, device_id_type=MESH)
    load_dense = pltpu.make_async_copy(dense_hbm, kept.at[core], load_sem.at[0])
    load_act = pltpu.make_async_copy(act_hbm, act.at[core], load_sem.at[1])
    load_goal = pltpu.make_async_copy(targets_hbm, goal, load_sem.at[2])
    load_dense.start()
    load_act.start()
    load_goal.start()

    def copy_to(src, dst, send, recv, device):
        pltpu.make_async_remote_copy(
            src_ref=src, dst_ref=dst, send_sem=send, recv_sem=recv, device_id=device, device_id_type=MESH
        ).start()

    def wait_for(ref, semaphore):
        pltpu.make_async_copy(ref, ref, semaphore).wait()

    contract_last = (((1,), (1,)), ((), ()))

    def first_product():
        load_dense.wait()
        load_act.wait()
        load_goal.wait()
        return lax.dot_general(
            kept[core].astype(jnp.bfloat16), act[core], contract_last, preferred_element_type=jnp.float32
        )

    def send_pieces(it):
        residuals = residual[it, core]
        arrival = sem.at[it, 14 - 11 * core]
        for dz, dx in COLUMN_PEERS:
            block, cx = lax.rem(z_lo + dz, 2), lax.rem(x + dx, 4)
            columns = pl.ds(pl.multiple_of(cx * PIECE_COLS, 128), PIECE_COLS)
            part = jnp.dot(residuals, act[block, :, columns], preferred_element_type=jnp.float32)
            for g in range(4):
                pieces[it, core, g * 8 + block * 4 + cx] = part[g * 8 : g * 8 + 8].astype(jnp.bfloat16)
            for dy in (2, 1, 3, 0):
                if (dy, dz, dx) != (0, 0, 0):
                    to = token_peer((dy, dz, dx))
                    copy_to(
                        pieces.at[it, core, to], arrived.at[it, core, tok], sem.at[it, 2], arrival,
                        {"feat": feat + 1 - core, "tok": to},
                    )

    def send_gradient(it, offsets):
        target = feat - core + jnp.where(it == ITERS - 1, z_lo, 1)
        for offset in TOKEN_PEERS:
            if offset[0] in offsets:
                copy_to(
                    gathered.at[it, tok], gathered.at[it, tok], sem.at[it, 6], sem.at[it, 7],
                    {"feat": target, "tok": token_peer(offset)},
                )

    def wait_for_last_gradient(it):
        @pl.when(z_lo == core)
        def _():
            wait_for(gathered.at[it, pl.ds(0, TOK // 2 - 1)], sem.at[it, 7])

        @pl.when(z_lo != core)
        def _():
            wait_for(gathered.at[it, pl.ds(0, TOK // 2)], sem.at[it, 7])

    def step_scale(lanes):
        total_square = jnp.sum(lanes, axis=1, keepdims=True)
        return step_size * lax.rsqrt(total_square / (ROWS * DIN) + epsilon)

    def shrunk_tile(it, scale, block, r, t):
        rows, columns = slice(r * 16, r * 16 + 16), slice(t * 128, t * 128 + 128)
        inner = slice((t % TILES) * 128, (t % TILES) * 128 + 128)
        gradient = gathered[it, r * 8 + block * 4 + t // TILES, :, inner].astype(jnp.float32)
        moved = ahead[block, rows, columns] - scale * gradient
        return rows, columns, moved - jnp.clip(moved, -threshold, threshold)

    def finish(it, scale, block):
        for t in range(4 * TILES):
            for r in range(4):
                rows, columns, shrunk = shrunk_tile(it, scale, block, r, t)
                weights[rows, columns] = shrunk

    @pl.when(core == 0)
    def _():
        pair_out[...] = first_product()
        pl.semaphore_wait(barrier, 1)
        copy_to(pair_out, pair_in, pair_sem.at[0], pair_sem.at[1], partner)
        copy_to(act.at[0], act.at[0], pair_sem.at[2], pair_sem.at[3], partner)
        copy_to(kept.at[0], kept.at[0], pair_sem.at[4], pair_sem.at[5], partner)
        wait_for(pair_out, pair_sem.at[0])
        wait_for(act.at[0], pair_sem.at[2])
        wait_for(act.at[1], pair_sem.at[3])

        def help_out(it, _):
            wait_for(residual.at[it, 0], sem.at[it, 11])
            send_pieces(it)
            copy_to(pieces.at[it, 0, tok], arrived.at[it, 0, tok], sem.at[it, 2], sem.at[it, 14], partner)
            wait_for(gathered.at[it, tok], sem.at[it, 13])
            send_gradient(it, AG_S)
            wait_for(pieces.at[it, 0], sem.at[it, 2])
            wait_for(gathered.at[it, pl.ds(0, 8 * len(AG_S) - (0 in AG_S))], sem.at[it, 6])
            return 0

        lax.fori_loop(0, ITERS, help_out, 0)
        wait_for(kept.at[0], pair_sem.at[4])
        wait_for(ahead.at[0], pair_sem.at[7])
        wait_for_last_gradient(ITERS - 1)
        wait_for(plane_sum, pair_sem.at[9])
        finish(ITERS - 1, step_scale(plane_sum[...]), 0)

    @pl.when(core == 1)
    def _():
        def line_peer(dz):
            to = lax.rem(z + dz, 8)
            return {"feat": (to // 2) * 2 + 1, "tok": y * 8 + lax.rem(to, 2) * 4 + x}

        momentum = momentum_terms(ITERS)
        factor = DIN ** (-0.5)
        product[...] = first_product()
        ahead[1] = kept[1]
        pl.semaphore_wait(barrier, TOK + FEAT // 2 - 1)
        copy_to(act.at[1], act.at[1], pair_sem.at[2], pair_sem.at[3], partner)
        wait_for(pair_in, pair_sem.at[1])
        product[...] += pair_in[...]

        def iteration(it, _):
            def s(i):
                return sem.at[it, i]

            own = product[...]
            part_out[it] = own.astype(jnp.bfloat16)
            for k in (2, 1, 3):
                copy_to(part_out.at[it], part_in.at[it, k - 1], s(0), s(1), {"feat": lax.rem(feat + 2 * k, FEAT)})

            @pl.when(it == ITERS - 1)
            def _():
                copy_to(ahead.at[0], ahead.at[0], pair_sem.at[6], pair_sem.at[7], partner)

            wait_for(part_in.at[it], s(1))
            for k in range(3):
                own = own + part_in[it, k].astype(jnp.float32)
            left = (factor * own - goal[...]).astype(jnp.bfloat16)
            for half in range(2):
                residual[it, half] = jnp.concatenate(
                    [left[g * 16 + half * 8 : g * 16 + half * 8 + 8] for g in range(4)], axis=0
                )
            copy_to(residual.at[it, 0], residual.at[it, 0], s(10), s(11), partner)

            @pl.when(it == 0)
            def _():
                wait_for(act.at[0], pair_sem.at[3])

            send_pieces(it)
            arrived[it, 1, tok] = pieces[it, 1, tok]

            @pl.when(it == 0)
            def _():
                wait_for(kept.at[0], pair_sem.at[5])
                ahead[0] = kept[0]

            def summed(half):
                total = arrived[it, half, 0].astype(jnp.float32)
                for p in range(1, TOK):
                    total = total + arrived[it, half, p].astype(jnp.float32)
                return total

            wait_for(arrived.at[it, 1, pl.ds(0, TOK - 1)], s(3))
            lower = summed(1)
            wait_for(arrived.at[it, 0], s(14))
            upper = summed(0)
            gathered[it, tok] = jnp.concatenate([upper, lower], axis=0).astype(jnp.bfloat16)
            copy_to(gathered.at[it, tok], gathered.at[it, tok], s(12), s(13), partner)
            square = upper * upper + lower * lower
            lanes = square[:, :128]
            for c in range(1, TILES):
                lanes = lanes + square[:, c * 128 : c * 128 + 128]

            def spread(squares, slot, value, send, recv, devices):
                squares[it, slot] = value
                for device in devices:
                    copy_to(squares.at[it, slot], squares.at[it, slot], send, recv, device)

            def collected(squares, recv, number):
                wait_for(squares.at[it, pl.ds(0, number - 1)], recv)
                sums = [squares[it, p] for p in range(number)]
                while len(sums) > 1:
                    sums = [a + b for a, b in zip(sums[::2], sums[1::2])]
                return sums[0]

            spread(
                line_squares, z, jnp.sum(lanes, axis=0, keepdims=True), s(4), s(5),
                [line_peer(dz) for dz in LINE_PEERS],
            )
            send_gradient(it, AG_N)
            spread(
                plane_squares, y * 4 + x, collected(line_squares, s(5), 8), s(8), s(9),
                [{"tok": token_peer((dy, 0, dx))} for dy, dx in PLANE_PEERS],
            )
            plane_sum[...] = collected(plane_squares, s(9), 16)

            @pl.when(it == ITERS - 1)
            def _():
                copy_to(plane_sum, plane_sum, pair_sem.at[8], pair_sem.at[9], partner)

            scale = step_scale(plane_sum[...])
            m = jnp.float32(momentum[0])
            for i in range(1, ITERS):
                m = jnp.where(it == i, jnp.float32(momentum[i]), m)
            @pl.when(it < ITERS - 1)
            def _():
                wait_for(gathered.at[it, pl.ds(0, TOK - 1)], s(7))
                total = None
                for block in range(2):
                    for chunk in range(7):
                        low = []
                        for r in range(4):
                            line = []
                            for t in range(chunk * 4, chunk * 4 + 4):
                                rows, columns, shrunk = shrunk_tile(it, scale, block, r, t)
                                advance = shrunk + m * (shrunk - kept[block, rows, columns])
                                kept[block, rows, columns] = shrunk
                                ahead[block, rows, columns] = advance
                                line.append(advance.astype(jnp.bfloat16))
                            low.append(jnp.concatenate(line, axis=1))
                        part = lax.dot_general(
                            jnp.concatenate(low, axis=0), act[block, :, chunk * 512 : chunk * 512 + 512],
                            contract_last, preferred_element_type=jnp.float32,
                        )
                        total = part if total is None else total + part
                product[...] = total

            @pl.when(it == ITERS - 1)
            def _():
                wait_for_last_gradient(it)
                finish(it, scale, 1)
                wait_for(ahead.at[0], pair_sem.at[6])
                wait_for(plane_sum, pair_sem.at[8])

            wait_for(part_in.at[it], s(0))
            wait_for(pieces.at[it, 1, pl.ds(0, TOK - 1)], s(2))
            wait_for(line_squares.at[it, pl.ds(0, 7)], s(4))
            wait_for(gathered.at[it, pl.ds(0, 8 * len(AG_N) - (0 in AG_N))], s(6))
            wait_for(residual.at[it, 0], s(10))
            wait_for(gathered.at[it, tok], s(12))
            wait_for(plane_squares.at[it, pl.ds(0, 15)], s(8))
            return 0

        lax.fori_loop(0, ITERS, iteration, 0)
        wait_for(act.at[1], pair_sem.at[2])


def shards(activations, dense_rows, targets):
    bf16, f32 = jnp.bfloat16, jnp.float32
    half_buffer = pltpu.VMEM((ITERS, 2, TOK, PIECE_ROWS // 2, PIECE_COLS), bf16)
    piece_buffer = pltpu.VMEM((ITERS, TOK, PIECE_ROWS, PIECE_COLS), bf16)
    return pl.pallas_call(
        kernel,
        out_shape=pltpu.VMEM((ROWS, COLS), f32),
        in_specs=[pl.BlockSpec(memory_space=pltpu.HBM)] * 3,
        out_specs=pl.BlockSpec(memory_space=pltpu.VMEM),
        scratch_shapes=[
            pltpu.VMEM((2, TOKENS, COLS), bf16),
            pltpu.VMEM((ROWS, TOKENS), f32),
            pltpu.VMEM((2, ROWS, COLS), f32),
            pltpu.VMEM((2, ROWS, COLS), f32),
            pltpu.VMEM((ROWS, TOKENS), f32),
            pltpu.VMEM((ROWS, TOKENS), f32),
            pltpu.VMEM((ROWS, TOKENS), f32),
            pltpu.VMEM((ITERS, ROWS, TOKENS), bf16),
            pltpu.VMEM((ITERS, 3, ROWS, TOKENS), bf16),
            pltpu.VMEM((ITERS, 2, ROWS // 2, TOKENS), bf16),
            half_buffer,
            half_buffer,
            piece_buffer,
            pltpu.VMEM((ITERS, 8, 1, 128), f32),
            pltpu.VMEM((ITERS, 16, 1, 128), f32),
            pltpu.VMEM((1, 128), f32),
            pltpu.SemaphoreType.DMA((3,)),
            pltpu.SemaphoreType.DMA((10,)),
            pltpu.SemaphoreType.DMA((ITERS, 15)),
        ],
        compiler_params=pltpu.CompilerParams(collective_id=0, has_side_effects=True),
    )(activations, dense_rows, targets.T)


def solution(mesh):
    in_specs = (P("tok", "feat"), P(None, "feat"), P("tok", None))
    out_specs = P(None, "feat")
    return jax.shard_map(shards, mesh=mesh, in_specs=in_specs, out_specs=out_specs, check_vma=False)
```

time: 103 us -> 101 us (0.981)
  Pallas kernels: 102 us -> 100 us
    pallas_call x1, Pallas kernels: 102 us -> 100 us  [shards(): pl.pallas_call(kernel, out_shape=pltpu.VMEM((ROWS, COLS), f32), in_specs=...]
where the time goes in v6:
time: 101 us
  Pallas kernels  100 us (99%)
    pallas_call x1, Pallas kernels, shards(): pl.pallas_call(kernel, out_shape=pltpu.VMEM((ROWS, COLS), f32), in_specs=...  100 us

profile of v6, /device:TPU:1, one launch (start us, length us, event | category | flops | bytes accessed | tf_op | source)
XLA Modules:
  0.0 101.2 jit_solution(11561097342863210700)
XLA Ops:
  0.0 100.2 %shard_map.37 = f32[64,3584]{1,0:T(8,128)S(1)} custom-call(bf16[256,3584]{1,0:T(8,128)(2,1)} %act_hbm.1, f32[64,3584]{1,0:T(8,128)} %dense_hbm.1, f32[64,256]{1,0:T(8,128)} %bitcast.1), custom_call_target="tpu_custom_call" | custom-call | tf_op jit(solution)/shard_map/pallas_call | solution.py:336
  100.2 0.9 copy.5

commit v7 on v6

--- a/solution.py
+++ b/solution.py
@@ -15,7 +15,6 @@
 threshold = 0.2
 epsilon = 1e-06
 
-AG_N, AG_S = (2,), (1, 3, 0)
 MESH = pl.DeviceIdType.MESH
 FEAT = 8
 TOK = 32
@@ -125,23 +124,24 @@
                         {"feat": feat + 1 - core, "tok": to},
                     )
 
-    def send_gradient(it, offsets):
+    def send_gradient(it):
         target = feat - core + jnp.where(it == ITERS - 1, z_lo, 1)
+        half = gathered.at[it, core, tok]
         for offset in TOKEN_PEERS:
-            if offset[0] in offsets:
-                copy_to(
-                    gathered.at[it, tok], gathered.at[it, tok], sem.at[it, 6], sem.at[it, 7],
-                    {"feat": target, "tok": token_peer(offset)},
-                )
+            copy_to(
+                half, half, sem.at[it, 6], sem.at[it, 15 - 8 * core], {"feat": target, "tok": token_peer(offset)}
+            )
 
     def wait_for_last_gradient(it):
         @pl.when(z_lo == core)
         def _():
-            wait_for(gathered.at[it, pl.ds(0, TOK // 2 - 1)], sem.at[it, 7])
+            wait_for(gathered.at[it, 1, pl.ds(0, TOK // 2 - 1)], sem.at[it, 7])
+            wait_for(gathered.at[it, 0, pl.ds(0, TOK // 2 - 1)], sem.at[it, 15])
 
         @pl.when(z_lo != core)
         def _():
-            wait_for(gathered.at[it, pl.ds(0, TOK // 2)], sem.at[it, 7])
+            wait_for(gathered.at[it, 1, pl.ds(0, TOK // 2)], sem.at[it, 7])
+            wait_for(gathered.at[it, 0, pl.ds(0, TOK // 2)], sem.at[it, 15])
 
     def step_scale(lanes):
         total_square = jnp.sum(lanes, axis=1, keepdims=True)
@@ -150,7 +150,10 @@
     def shrunk_tile(it, scale, block, r, t):
         rows, columns = slice(r * 16, r * 16 + 16), slice(t * 128, t * 128 + 128)
         inner = slice((t % TILES) * 128, (t % TILES) * 128 + 128)
-        gradient = gathered[it, r * 8 + block * 4 + t // TILES, :, inner].astype(jnp.float32)
+        gradient = jnp.concatenate(
+            [gathered[it, half, r * 8 + block * 4 + t // TILES, :, inner].astype(jnp.float32) for half in range(2)],
+            axis=0,
+        )
         moved = ahead[block, rows, columns] - scale * gradient
         return rows, columns, moved - jnp.clip(moved, -threshold, threshold)
 
@@ -175,10 +178,11 @@
             wait_for(residual.at[it, 0], sem.at[it, 11])
             send_pieces(it)
             copy_to(pieces.at[it, 0, tok], arrived.at[it, 0, tok], sem.at[it, 2], sem.at[it, 14], partner)
-            wait_for(gathered.at[it, tok], sem.at[it, 13])
-            send_gradient(it, AG_S)
+            wait_for(gathered.at[it, 0, tok], sem.at[it, 13])
+            send_gradient(it)
+            wait_for(gathered.at[it, 1, tok], sem.at[it, 16])
             wait_for(pieces.at[it, 0], sem.at[it, 2])
-            wait_for(gathered.at[it, pl.ds(0, 8 * len(AG_S) - (0 in AG_S))], sem.at[it, 6])
+            wait_for(gathered.at[it, 0, pl.ds(0, TOK - 1)], sem.at[it, 6])
             return 0
 
         lax.fori_loop(0, ITERS, help_out, 0)
@@ -246,10 +250,13 @@
 
             wait_for(arrived.at[it, 1, pl.ds(0, TOK - 1)], s(3))
             lower = summed(1)
+            gathered[it, 1, tok] = lower.astype(jnp.bfloat16)
+            send_gradient(it)
+            copy_to(gathered.at[it, 1, tok], gathered.at[it, 1, tok], s(17), s(16), partner)
             wait_for(arrived.at[it, 0], s(14))
             upper = summed(0)
-            gathered[it, tok] = jnp.concatenate([upper, lower], axis=0).astype(jnp.bfloat16)
-            copy_to(gathered.at[it, tok], gathered.at[it, tok], s(12), s(13), partner)
+            gathered[it, 0, tok] = upper.astype(jnp.bfloat16)
+            copy_to(gathered.at[it, 0, tok], gathered.at[it, 0, tok], s(12), s(13), partner)
             square = upper * upper + lower * lower
             lanes = square[:, :128]
             for c in range(1, TILES):
@@ -271,7 +278,6 @@
                 line_squares, z, jnp.sum(lanes, axis=0, keepdims=True), s(4), s(5),
                 [line_peer(dz) for dz in LINE_PEERS],
             )
-            send_gradient(it, AG_N)
             spread(
                 plane_squares, y * 4 + x, collected(line_squares, s(5), 8), s(8), s(9),
                 [{"tok": token_peer((dy, 0, dx))} for dy, dx in PLANE_PEERS],
@@ -288,7 +294,8 @@
                 m = jnp.where(it == i, jnp.float32(momentum[i]), m)
             @pl.when(it < ITERS - 1)
             def _():
-                wait_for(gathered.at[it, pl.ds(0, TOK - 1)], s(7))
+                wait_for(gathered.at[it, 1, pl.ds(0, TOK - 1)], s(7))
+                wait_for(gathered.at[it, 0, pl.ds(0, TOK - 1)], s(15))
                 total = None
                 for block in range(2):
                     for chunk in range(7):
@@ -319,9 +326,10 @@
             wait_for(part_in.at[it], s(0))
             wait_for(pieces.at[it, 1, pl.ds(0, TOK - 1)], s(2))
             wait_for(line_squares.at[it, pl.ds(0, 7)], s(4))
-            wait_for(gathered.at[it, pl.ds(0, 8 * len(AG_N) - (0 in AG_N))], s(6))
+            wait_for(gathered.at[it, 1, pl.ds(0, TOK - 1)], s(6))
+            wait_for(gathered.at[it, 1, tok], s(17))
             wait_for(residual.at[it, 0], s(10))
-            wait_for(gathered.at[it, tok], s(12))
+            wait_for(gathered.at[it, 0, tok], s(12))
             wait_for(plane_squares.at[it, pl.ds(0, 15)], s(8))
             return 0
 
@@ -332,7 +340,6 @@
 def shards(activations, dense_rows, targets):
     bf16, f32 = jnp.bfloat16, jnp.float32
     half_buffer = pltpu.VMEM((ITERS, 2, TOK, PIECE_ROWS // 2, PIECE_COLS), bf16)
-    piece_buffer = pltpu.VMEM((ITERS, TOK, PIECE_ROWS, PIECE_COLS), bf16)
     return pl.pallas_call(
         kernel,
         out_shape=pltpu.VMEM((ROWS, COLS), f32),
@@ -351,13 +358,13 @@
             pltpu.VMEM((ITERS, 2, ROWS // 2, TOKENS), bf16),
             half_buffer,
             half_buffer,
-            piece_buffer,
+            half_buffer,
             pltpu.VMEM((ITERS, 8, 1, 128), f32),
             pltpu.VMEM((ITERS, 16, 1, 128), f32),
             pltpu.VMEM((1, 128), f32),
             pltpu.SemaphoreType.DMA((3,)),
             pltpu.SemaphoreType.DMA((10,)),
-            pltpu.SemaphoreType.DMA((ITERS, 15)),
+            pltpu.SemaphoreType.DMA((ITERS, 18)),
         ],
         compiler_params=pltpu.CompilerParams(collective_id=0, has_side_effects=True),
     )(activations, dense_rows, targets.T)

time: 101 us -> 110 us (1.089)
  Pallas kernels: 100 us -> 109 us
    pallas_call x1, Pallas kernels: 100 us -> 109 us  [shards(): pl.pallas_call(kernel, out_shape=pltpu.VMEM((ROWS, COLS), f32), in_specs=...]
where the time goes in v7:
time: 110 us
  Pallas kernels  109 us (99%)
    pallas_call x1, Pallas kernels, shards(): pl.pallas_call(kernel, out_shape=pltpu.VMEM((ROWS, COLS), f32), in_specs=...  109 us

profile of v7, /device:TPU:1, one launch (start us, length us, event | category | flops | bytes accessed | tf_op | source)
XLA Modules:
  0.0 110.2 jit_solution(9153178732822267679)
XLA Ops:
  0.0 109.3 %shard_map.37 = f32[64,3584]{1,0:T(8,128)S(1)} custom-call(bf16[256,3584]{1,0:T(8,128)(2,1)} %act_hbm.1, f32[64,3584]{1,0:T(8,128)} %dense_hbm.1, f32[64,256]{1,0:T(8,128)} %bitcast.1), custom_call_target="tpu_custom_call" | custom-call | tf_op jit(solution)/shard_map/pallas_call | solution.py:343
  109.3 0.9 copy.5
